TPU v7x, 32 devices: a whole 2x2x4 slice. The times are simulated.
32 devices in a mesh: gx: 2 (over core), gy: 4 (over y, x), ma: 4 (over z).
Axes of the slice: x: 2, y: 2, z: 4, core: 2. Of those that a mesh axis runs over, the one named last changes fastest.
Arguments:
- object_field: float32 [2, 256, 1024], P(None, 'gx', 'gy'), may hold values from -5 to 5
- probe_modes: float32 [8, 2, 256, 256], P('ma'), may hold values from -1.5 to 1.5
- measured: float32 [2, 4, 2, 256, 256], P('gx', 'gy'), may hold values from 0.1 to 4
- positions: int32 [2, 4, 2, 2], P('gx', 'gy'), may hold values from 0 to 255, as said below
- slot_counts: int32 [2, 4], P('gx', 'gy'), may hold values from 1 to 2, as said below
Outputs:
- updated_object: float32 [2, 256, 1024], P(None, 'gx', 'gy')
Inputs may be any that keep to these rules, and one draw needn't show every extreme that they name: positions[a, b, s] holds a row 0 to 127 and a column 0 to 255 of tile (a, b); slots s >= slot_counts[a, b] are unused. `slot_counts`: some tile uses all 2 slots.
All inputs are finite; a program needn't handle non-finite values.
Results may differ from a plain program's by a relative error of at most 0.0023.
Values sent between devices are 32-bit elements; how exact they have to be, the bound alone decides.
A program may use at most 64 MiB of HBM per device.

v0:
```python
import math

import jax
import jax.numpy as jnp
from jax import lax
from jax.sharding import PartitionSpec as P

OUTER = 2


DAMPING = 1.0


def padded_2(block, sides, width):
    for axis, dim in sides:
        count = lax.axis_size(axis)
        forward = [(i, i + 1) for i in range(count - 1)]
        backward = [(target, source) for source, target in forward]
        low = lax.ppermute(
            lax.slice_in_dim(block, block.shape[dim] - width, None, axis=dim), axis, forward
        )
        high = lax.ppermute(lax.slice_in_dim(block, 0, width, axis=dim), axis, backward)
        block = jnp.concatenate([low, block, high], axis=dim)
    return block


def dft_tables(patch_width):
    ladder = jnp.arange(patch_width, dtype=jnp.int32)
    phases = ladder[:, None] * ladder[None, :] % patch_width
    angles = phases.astype(jnp.float32) * (2.0 * math.pi / patch_width)
    factor = 1.0 / math.sqrt(patch_width)
    real_part = jnp.cos(angles) * factor
    imag_part = -jnp.sin(angles) * factor
    table_one = jnp.concatenate(
        [jnp.concatenate([real_part, -imag_part], 1), jnp.concatenate([imag_part, real_part], 1)], 0
    ).astype(jnp.bfloat16)
    table_two = jnp.concatenate(
        [jnp.concatenate([real_part, imag_part], 1), jnp.concatenate([-imag_part, real_part], 1)], 0
    ).astype(jnp.bfloat16)
    return (table_one, table_two)


def forward_transform(wavefield, tables):
    patch_width = wavefield.shape[-1]
    halfway = jnp.einsum(
        "pqci,bcik->bpqk",
        tables[0].reshape(2, patch_width, 2, patch_width),
        wavefield,
        preferred_element_type=jnp.float32,
    ).astype(jnp.bfloat16)
    return jnp.einsum(
        "bcik,ckl->bil",
        halfway,
        tables[1].reshape(2, patch_width, 2 * patch_width),
        preferred_element_type=jnp.float32,
    )


def adjoint_transform(weighted, tables):
    patch_width = weighted.shape[1]
    halfway = jnp.einsum(
        "bik,kl->bil", weighted, tables[0], preferred_element_type=jnp.float32
    ).astype(jnp.bfloat16)
    return jnp.einsum(
        "pqci,bicl->bpql",
        tables[1].reshape(2, patch_width, 2, patch_width),
        halfway.reshape(halfway.shape[0], patch_width, 2, patch_width),
        preferred_element_type=jnp.float32,
    )


def exit_waves(probe_modes, windows):
    probe_real = probe_modes[None, :, 0]
    probe_imag = probe_modes[None, :, 1]
    window_real = windows[:, None, 0]
    window_imag = windows[:, None, 1]
    real_part = probe_real * window_real - probe_imag * window_imag
    imag_part = probe_real * window_imag + probe_imag * window_real
    wavefield = jnp.stack([real_part, imag_part], 2).astype(jnp.bfloat16)
    return wavefield.reshape(-1, 2, probe_modes.shape[-1], probe_modes.shape[-1])


def intensity_part(spectra, mode_count):
    patch_width = spectra.shape[1]
    grouped = spectra.reshape(-1, mode_count, patch_width, 2 * patch_width)
    squared = grouped * grouped
    return jnp.sum(squared[..., :patch_width] + squared[..., patch_width:], axis=1)


def change_part(spectra, moved_spectra, mode_count):
    patch_width = spectra.shape[1]
    grouped = spectra.reshape(-1, mode_count, patch_width, 2 * patch_width)
    shifted = moved_spectra.reshape(-1, mode_count, patch_width, 2 * patch_width)
    product = grouped * shifted
    return 2.0 * jnp.sum(product[..., :patch_width] + product[..., patch_width:], axis=1)


def mode_images(weights, spectra, probe_modes, tables):
    mode_count = probe_modes.shape[0]
    patch_width = probe_modes.shape[-1]
    doubled = jnp.concatenate([weights, weights], -1)
    grouped = spectra.reshape(-1, mode_count, patch_width, 2 * patch_width)
    weighted = (2.0 * grouped * doubled[:, None]).astype(jnp.bfloat16)
    returned = adjoint_transform(weighted.reshape(-1, patch_width, 2 * patch_width), tables)
    returned = returned.reshape(-1, mode_count, 2, patch_width, patch_width)
    probe_real = probe_modes[None, :, 0]
    probe_imag = probe_modes[None, :, 1]
    real_part = jnp.sum(probe_real * returned[:, :, 0] + probe_imag * returned[:, :, 1], axis=1)
    imag_part = jnp.sum(probe_real * returned[:, :, 1] - probe_imag * returned[:, :, 0], axis=1)
    return jnp.stack([real_part, imag_part], 1)


def fold_edges(widened, axis_dim, length, rim_width):
    middle = lax.slice_in_dim(widened, 2 * rim_width, 2 * rim_width + length, axis=axis_dim)
    low_rim = lax.slice_in_dim(widened, 0, rim_width, axis=axis_dim)
    high_rim = lax.slice_in_dim(
        widened, length + 3 * rim_width, length + 4 * rim_width, axis=axis_dim
    )
    low_pads = [(0, 0), (0, 0), (0, 0)]
    high_pads = [(0, 0), (0, 0), (0, 0)]
    low_pads[axis_dim] = (0, length - rim_width)
    high_pads[axis_dim] = (length - rim_width, 0)
    return middle + jnp.pad(low_rim, low_pads) + jnp.pad(high_rim, high_pads)


def shards(object_field, probe_modes, measured, positions, slot_counts):
    patch_width = probe_modes.shape[-1]
    mode_count = probe_modes.shape[0]
    rim_width = patch_width // 2
    tile_rows = object_field.shape[1]
    tile_cols = object_field.shape[2]
    slot_count = measured.shape[2]
    share_rows = tile_rows // lax.axis_size("ma")
    tables = dft_tables(patch_width)
    targets = measured[0, 0]
    centres = positions[0, 0]
    live_mask = (jnp.arange(slot_count, dtype=jnp.int32) < slot_counts[0, 0]).astype(jnp.float32)[
        :, None, None
    ]
    anchor = jnp.zeros((), jnp.int32)

    def spectra_of(current):
        padded = padded_2(current, (("gx", 1), ("gy", 2)), rim_width)
        windows = jnp.stack(
            [
                lax.dynamic_slice(
                    padded,
                    (anchor, centres[slot_index, 0], centres[slot_index, 1]),
                    (2, patch_width, patch_width),
                )
                for slot_index in range(slot_count)
            ],
            0,
        )
        return forward_transform(exit_waves(probe_modes, windows), tables)

    def mode_total(partial_value):
        return lax.psum(partial_value, "ma")

    def combine(folded):
        summed = lax.psum(folded, "ma")
        return summed

    def project(weights, spectra):
        pieces = mode_images(weights, spectra, probe_modes, tables)
        extended = jnp.zeros((2, tile_rows + patch_width, tile_cols + patch_width), jnp.float32)
        for slot_index in range(slot_count):
            corner = (anchor, centres[slot_index, 0], centres[slot_index, 1])
            extended = lax.dynamic_update_slice(
                extended,
                lax.dynamic_slice(extended, corner, (2, patch_width, patch_width))
                + pieces[slot_index],
                corner,
            )
        widened = padded_2(extended, (("gx", 1), ("gy", 2)), rim_width)
        folded = fold_edges(fold_edges(widened, 1, tile_rows, rim_width), 2, tile_cols, rim_width)
        result = combine(folded)
        return result

    def local_sum(first_vec, second_vec):
        first_vec = lax.dynamic_slice_in_dim(
            first_vec, lax.axis_index("ma") * share_rows, share_rows, 1
        )
        second_vec = lax.dynamic_slice_in_dim(
            second_vec, lax.axis_index("ma") * share_rows, share_rows, 1
        )
        return jnp.sum(first_vec * second_vec)

    current = object_field
    for outer_step in range(OUTER):
        spectra = spectra_of(current)
        misfit = live_mask * (mode_total(intensity_part(spectra, mode_count)) - targets)
        gradient = project(misfit, spectra)
        residual = -gradient
        direction = residual
        norm_now = lax.psum(local_sum(residual, residual), ("gx", "gy", "ma"))
        moved_spectra = spectra_of(direction)
        change = live_mask * mode_total(change_part(spectra, moved_spectra, mode_count))
        applied = project(change, spectra) + DAMPING * direction
        step_size = norm_now / lax.psum(local_sum(direction, applied), ("gx", "gy", "ma"))
        update = step_size * direction
        residual = residual - step_size * applied
        current = current + update
    return current


def solution(mesh):
    return jax.shard_map(
        shards,
        mesh=mesh,
        in_specs=(
            P(None, "gx", "gy"),
            P("ma", None, None, None),
            P("gx", "gy", None, None, None),
            P("gx", "gy", None, None),
            P("gx", "gy"),
        ),
        out_specs=P(None, "gx", "gy"),
        check_vma=False,
    )
```

profile of v0, /device:TPU:0, one launch (start us, length us, event | category | flops | bytes accessed | tf_op | source)
XLA Modules:
  0.0 795.4 jit_solution(15070351154825093424)
XLA Ops:
  45.2 36.4 %all-reduce.15.cloned.1.call-done = f32[2,256,256]{2,1,0:T(8,128)} async-done(((f32[2,256,256]{2,1,0:T(8,128)}), f32[2,256,256]{2,1,0:T(8,128)}) %all-reduce.15.cloned.1.call-update) | async-done | bytes 524304 | tf_op jit(solution)/shard_map/psum | solution.py:158
  89.5 8.2 %dynamic_update_slice.24 = f32[2,384,512]{1,2,0:T(8,128)S(1)} dynamic-update-slice(f32[2,384,512]{1,2,0:T(8,128)S(1)} %broadcast.214.clone.1, f32[2,256,256]{1,2,0:T(8,128)} %fusion.37, s32[]{:T(128)} %constant.15.clone.1, s32[]{:T(128)S(6)} %select_n.31, s32[]{:T(128)S(6)} %select_n.32) | dynamic-update-slice | bytes 1048580 | tf_op jit(solution)/shard_map/dynamic_update_slice | solution.py:169
  116.8 12.9 %collective-permute-done.6 = f32[2,640,128]{1,2,0:T(8,128)S(1)} collective-permute-done((f32[2,640,128]{1,2,0:T(8,128)S(1)}, f32[2,640,128]{1,2,0:T(8,128)S(1)}, u32[]{:S(2)}, u32[]{:S(2)}) %collective-permute-start.6) | collective-permute-done | bytes 655392 | tf_op jit(solution)/shard_map/ppermute | solution.py:19
  129.7 16.1 %collective-permute-done.7 = f32[2,640,128]{1,2,0:T(8,128)S(1)} collective-permute-done((f32[2,640,128]{1,2,0:T(8,128)S(1)}, f32[2,640,128]{1,2,0:T(8,128)S(1)}, u32[]{:S(2)}, u32[]{:S(2)}) %collective-permute-start.7) | collective-permute-done | bytes 655392 | tf_op jit(solution)/shard_map/ppermute | solution.py:22
  147.3 34.6 %all-reduce.17.cloned.1.call-done = f32[2,128,256]{1,2,0:T(8,128)} async-done(((f32[2,128,256]{1,2,0:T(8,128)}), f32[2,128,256]{1,2,0:T(8,128)}) %all-reduce.17.cloned.1.call-update) | async-done | bytes 262160 | tf_op jit(solution)/shard_map/psum | solution.py:161
  199.9 10.3 %collective-permute-done.11 = f32[2,384,128]{1,2,0:T(8,128)S(1)} collective-permute-done((f32[2,384,128]{1,2,0:T(8,128)S(1)}, f32[2,384,128]{1,2,0:T(8,128)S(1)}, u32[]{:S(2)}, u32[]{:S(2)}) %collective-permute-start.11) | collective-permute-done | bytes 393248 | tf_op jit(solution)/shard_map/ppermute | solution.py:22
  218.0 37.6 %all-reduce.19.cloned.1.call-done = f32[2,256,256]{2,1,0:T(8,128)} async-done(((f32[2,256,256]{2,1,0:T(8,128)}), f32[2,256,256]{2,1,0:T(8,128)}) %all-reduce.19.cloned.1.call-update) | async-done | bytes 524304 | tf_op jit(solution)/shard_map/psum | solution.py:158
  263.3 8.2 %dynamic_update_slice.26 = f32[2,384,512]{1,2,0:T(8,128)S(1)} dynamic-update-slice(f32[2,384,512]{1,2,0:T(8,128)S(1)} %broadcast.214.clone, f32[2,256,256]{1,2,0:T(8,128)} %fusion.33, s32[]{:T(128)} %constant.15.clone.1, s32[]{:T(128)S(6)} %select_n.31, s32[]{:T(128)S(6)} %select_n.32) | dynamic-update-slice | bytes 1048580 | tf_op jit(solution)/shard_map/dynamic_update_slice | solution.py:169
  290.6 12.9 %collective-permute-done.14 = f32[2,640,128]{1,2,0:T(8,128)S(1)} collective-permute-done((f32[2,640,128]{1,2,0:T(8,128)S(1)}, f32[2,640,128]{1,2,0:T(8,128)S(1)}, u32[]{:S(2)}, u32[]{:S(2)}) %collective-permute-start.14) | collective-permute-done | bytes 655392 | tf_op jit(solution)/shard_map/ppermute | solution.py:19
  303.6 16.1 %collective-permute-done.15 = f32[2,640,128]{1,2,0:T(8,128)S(1)} collective-permute-done((f32[2,640,128]{1,2,0:T(8,128)S(1)}, f32[2,640,128]{1,2,0:T(8,128)S(1)}, u32[]{:S(2)}, u32[]{:S(2)}) %collective-permute-start.15) | collective-permute-done | bytes 655392 | tf_op jit(solution)/shard_map/ppermute | solution.py:22
  320.8 34.5 %all-reduce.21.cloned.1.call-done = f32[2,128,256]{1,2,0:T(8,128)} async-done(((f32[2,128,256]{1,2,0:T(8,128)}), f32[2,128,256]{1,2,0:T(8,128)}) %all-reduce.21.cloned.1.call-update) | async-done | bytes 262160 | tf_op jit(solution)/shard_map/psum | solution.py:161
  357.1 40.4 %all-reduce.5 = (f32[]{:T(128)}, f32[]{:T(128)}) all-reduce(f32[]{:T(128)} %get-tuple-element.16, f32[]{:T(128)} %get-tuple-element.15), channel_id=1, replica_groups=mesh['gx'=2,'gy'=4,'ma'=4] {'gx','gy','ma'}, use_global_device_ids=true, to_apply=%region_6.7 | all-reduce | flops 2 | bytes 16 | tf_op jit(solution)/shard_map/psum | solution.py:196
  416.6 10.6 %collective-permute-done.19 = f32[2,384,128]{1,2,0:T(8,128)S(1)} collective-permute-done((f32[2,384,128]{1,2,0:T(8,128)S(1)}, f32[2,384,128]{1,2,0:T(8,128)S(1)}, u32[]{:S(2)}, u32[]{:S(2)}) %collective-permute-start.19) | collective-permute-done | bytes 393248 | tf_op jit(solution)/shard_map/ppermute | solution.py:22
  434.6 36.3 %all-reduce.23.cloned.1.call-done = f32[2,256,256]{2,1,0:T(8,128)} async-done(((f32[2,256,256]{2,1,0:T(8,128)}), f32[2,256,256]{2,1,0:T(8,128)}) %all-reduce.23.cloned.1.call-update) | async-done | bytes 524304 | tf_op jit(solution)/shard_map/psum | solution.py:158
  506.1 12.9 %collective-permute-done.22 = f32[2,640,128]{1,2,0:T(8,128)S(1)} collective-permute-done((f32[2,640,128]{1,2,0:T(8,128)S(1)}, f32[2,640,128]{1,2,0:T(8,128)S(1)}, u32[]{:S(2)}, u32[]{:S(2)}) %collective-permute-start.22) | collective-permute-done | bytes 655392 | tf_op jit(solution)/shard_map/ppermute | solution.py:19
  519.0 16.1 %collective-permute-done.23 = f32[2,640,128]{1,2,0:T(8,128)S(1)} collective-permute-done((f32[2,640,128]{1,2,0:T(8,128)S(1)}, f32[2,640,128]{1,2,0:T(8,128)S(1)}, u32[]{:S(2)}, u32[]{:S(2)}) %collective-permute-start.23) | collective-permute-done | bytes 655392 | tf_op jit(solution)/shard_map/ppermute | solution.py:22
  536.1 34.6 %all-reduce.25.cloned.1.call-done = f32[2,128,256]{1,2,0:T(8,128)} async-done(((f32[2,128,256]{1,2,0:T(8,128)}), f32[2,128,256]{1,2,0:T(8,128)}) %all-reduce.25.cloned.1.call-update) | async-done | bytes 262160 | tf_op jit(solution)/shard_map/psum | solution.py:161
  588.6 10.3 %collective-permute-done.27 = f32[2,384,128]{1,2,0:T(8,128)S(1)} collective-permute-done((f32[2,384,128]{1,2,0:T(8,128)S(1)}, f32[2,384,128]{1,2,0:T(8,128)S(1)}, u32[]{:S(2)}, u32[]{:S(2)}) %collective-permute-start.27) | collective-permute-done | bytes 393248 | tf_op jit(solution)/shard_map/ppermute | solution.py:22
  606.7 37.6 %all-reduce.27.cloned.1.call-done = f32[2,256,256]{2,1,0:T(8,128)} async-done(((f32[2,256,256]{2,1,0:T(8,128)}), f32[2,256,256]{2,1,0:T(8,128)}) %all-reduce.27.cloned.1.call-update) | async-done | bytes 524304 | tf_op jit(solution)/shard_map/psum | solution.py:158
  651.8 8.8 %dynamic_update_slice.30 = f32[2,384,512]{1,2,0:T(8,128)S(1)} dynamic-update-slice(f32[2,384,512]{1,2,0:T(8,128)S(1)} %broadcast.214, f32[2,256,256]{1,2,0:T(8,128)S(1)} %fusion.25, s32[]{:T(128)} %constant.15.clone.1, s32[]{:T(128)S(6)} %select_n.31, s32[]{:T(128)S(6)} %select_n.32) | dynamic-update-slice | bytes 1048580 | tf_op jit(solution)/shard_map/dynamic_update_slice | solution.py:169
  679.0 12.9 %collective-permute-done.30 = f32[2,640,128]{1,2,0:T(8,128)S(1)} collective-permute-done((f32[2,640,128]{1,2,0:T(8,128)S(1)}, f32[2,640,128]{1,2,0:T(8,128)S(1)}, u32[]{:S(2)}, u32[]{:S(2)}) %collective-permute-start.30) | collective-permute-done | bytes 655392 | tf_op jit(solution)/shard_map/ppermute | solution.py:19
  691.9 16.0 %collective-permute-done.31 = f32[2,640,128]{1,2,0:T(8,128)S(1)} collective-permute-done((f32[2,640,128]{1,2,0:T(8,128)S(1)}, f32[2,640,128]{1,2,0:T(8,128)S(1)}, u32[]{:S(2)}, u32[]{:S(2)}) %collective-permute-start.31) | collective-permute-done | bytes 655392 | tf_op jit(solution)/shard_map/ppermute | solution.py:22
  709.0 34.7 %all-reduce.29.cloned.1.call-done = f32[2,128,256]{1,2,0:T(8,128)} async-done(((f32[2,128,256]{1,2,0:T(8,128)}), f32[2,128,256]{1,2,0:T(8,128)}) %all-reduce.29.cloned.1.call-update) | async-done | bytes 262160 | tf_op jit(solution)/shard_map/psum | solution.py:161
  745.5 40.4 %all-reduce.4 = (f32[]{:T(128)}, f32[]{:T(128)}) all-reduce(f32[]{:T(128)} %get-tuple-element.14, f32[]{:T(128)} %get-tuple-element.13), channel_id=1, replica_groups=mesh['gx'=2,'gy'=4,'ma'=4] {'gx','gy','ma'}, use_global_device_ids=true, to_apply=%region_20.21 | all-reduce | flops 2 | bytes 16 | tf_op jit(solution)/shard_map/psum | solution.py:196
  (272 shorter events, 229.6 us)
Async XLA Ops:
  6.5 75.1 %all-reduce.15.cloned.1.call-start = ((), (), s32[]{:S(2)}) async-start(), calls=%async_computation | async-start | bytes 1048576 | tf_op jit(solution)/shard_map/psum | solution.py:158
  13.7 17.3 %collective-permute-start.2 = (f32[2,384,128]{2,1,0:T(8,128)}, f32[2,384,128]{2,1,0:T(8,128)S(1)}, u32[]{:S(2)}, u32[]{:S(2)}) collective-permute-start(f32[2,384,128]{2,1,0:T(8,128)} %get-tuple-element.69), channel_id=1, source_target_pairs={{0,4},{4,8},{8,12},{1,5},{5,9},{9,13},{2,6},{6,10},{10,14},{3,7},{... | collective-permute-start | bytes 1179656 | tf_op jit(solution)/shard_map/ppermute | solution.py:19
  17.9 19.4 %collective-permute-start.3 = (f32[2,384,128]{2,1,0:T(8,128)}, f32[2,384,128]{2,1,0:T(8,128)}, u32[]{:S(2)}, u32[]{:S(2)}) collective-permute-start(f32[2,384,128]{2,1,0:T(8,128)} %get-tuple-element.70), channel_id=1, source_target_pairs={{4,0},{8,4},{12,8},{5,1},{9,5},{13,9},{6,2},{10,6},{14,10},{7,3},{... | collective-permute-start | bytes 1179656 | tf_op jit(solution)/shard_map/ppermute | solution.py:22
  42.5 139.5 %all-reduce.17.cloned.1.call-start = ((), (), s32[]{:S(2)}) async-start(), calls=%async_computation.1 | async-start | bytes 524288 | tf_op jit(solution)/shard_map/psum | solution.py:161
  112.0 17.7 %collective-permute-start.6 = (f32[2,640,128]{1,2,0:T(8,128)S(1)}, f32[2,640,128]{1,2,0:T(8,128)S(1)}, u32[]{:S(2)}, u32[]{:S(2)}) collective-permute-start(f32[2,640,128]{1,2,0:T(8,128)S(1)} %get-tuple-element.27), channel_id=1, source_target_pairs={{0,4},{4,8},{8,12},{1,5},{5,9},{9,13},{2,6},{6,10},{10,14},{3,7},{... | collective-permute-start | bytes 1966088 | tf_op jit(solution)/shard_map/ppermute | solution.py:19
  115.5 30.3 %collective-permute-start.7 = (f32[2,640,128]{1,2,0:T(8,128)S(1)}, f32[2,640,128]{1,2,0:T(8,128)S(1)}, u32[]{:S(2)}, u32[]{:S(2)}) collective-permute-start(f32[2,640,128]{1,2,0:T(8,128)S(1)} %get-tuple-element.28), channel_id=1, source_target_pairs={{4,0},{8,4},{12,8},{5,1},{9,5},{13,9},{6,2},{10,6},{14,10},{7,3},{... | collective-permute-start | bytes 1966088 | tf_op jit(solution)/shard_map/ppermute | solution.py:22
  147.3 108.3 %all-reduce.19.cloned.1.call-start = ((), (), s32[]{:S(2)}) async-start(), calls=%async_computation.2 | async-start | bytes 1048576 | tf_op jit(solution)/shard_map/psum | solution.py:158
  187.8 12.0 %collective-permute-start.10 = (f32[2,384,128]{1,2,0:T(8,128)S(1)}, f32[2,384,128]{1,2,0:T(8,128)S(1)}, u32[]{:S(2)}, u32[]{:S(2)}) collective-permute-start(f32[2,384,128]{1,2,0:T(8,128)S(1)} %get-tuple-element.67), channel_id=1, source_target_pairs={{0,4},{4,8},{8,12},{1,5},{5,9},{9,13},{2,6},{6,10},{10,14},{3,7},{... | collective-permute-start | bytes 1179656 | tf_op jit(solution)/shard_map/ppermute | solution.py:19
  191.2 19.0 %collective-permute-start.11 = (f32[2,384,128]{1,2,0:T(8,128)S(1)}, f32[2,384,128]{1,2,0:T(8,128)S(1)}, u32[]{:S(2)}, u32[]{:S(2)}) collective-permute-start(f32[2,384,128]{1,2,0:T(8,128)S(1)} %get-tuple-element.68), channel_id=1, source_target_pairs={{4,0},{8,4},{12,8},{5,1},{9,5},{13,9},{6,2},{10,6},{14,10},{7,3},{... | collective-permute-start | bytes 1179656 | tf_op jit(solution)/shard_map/ppermute | solution.py:22
  217.9 137.4 %all-reduce.21.cloned.1.call-start = ((), (), s32[]{:S(2)}) async-start(), calls=%async_computation.3 | async-start | bytes 524288 | tf_op jit(solution)/shard_map/psum | solution.py:161
  285.9 17.7 %collective-permute-start.14 = (f32[2,640,128]{1,2,0:T(8,128)S(1)}, f32[2,640,128]{1,2,0:T(8,128)S(1)}, u32[]{:S(2)}, u32[]{:S(2)}) collective-permute-start(f32[2,640,128]{1,2,0:T(8,128)S(1)} %get-tuple-element.25), channel_id=1, source_target_pairs={{0,4},{4,8},{8,12},{1,5},{5,9},{9,13},{2,6},{6,10},{10,14},{3,7},{... | collective-permute-start | bytes 1966088 | tf_op jit(solution)/shard_map/ppermute | solution.py:19
  289.3 30.3 %collective-permute-start.15 = (f32[2,640,128]{1,2,0:T(8,128)S(1)}, f32[2,640,128]{1,2,0:T(8,128)S(1)}, u32[]{:S(2)}, u32[]{:S(2)}) collective-permute-start(f32[2,640,128]{1,2,0:T(8,128)S(1)} %get-tuple-element.26), channel_id=1, source_target_pairs={{4,0},{8,4},{12,8},{5,1},{9,5},{13,9},{6,2},{10,6},{14,10},{7,3},{... | collective-permute-start | bytes 1966088 | tf_op jit(solution)/shard_map/ppermute | solution.py:22
  320.6 150.3 %all-reduce.23.cloned.1.call-start = ((), (), s32[]{:S(2)}) async-start(), calls=%async_computation.4 | async-start | bytes 1048576 | tf_op jit(solution)/shard_map/psum | solution.py:158
  403.8 12.8 %collective-permute-start.18 = (f32[2,384,128]{1,2,0:T(8,128)S(1)}, f32[2,384,128]{1,2,0:T(8,128)S(1)}, u32[]{:S(2)}, u32[]{:S(2)}) collective-permute-start(f32[2,384,128]{1,2,0:T(8,128)S(1)} %get-tuple-element.65), channel_id=1, source_target_pairs={{0,4},{4,8},{8,12},{1,5},{5,9},{9,13},{2,6},{6,10},{10,14},{3,7},{... | collective-permute-start | bytes 1179656 | tf_op jit(solution)/shard_map/ppermute | solution.py:19
  408.0 19.2 %collective-permute-start.19 = (f32[2,384,128]{1,2,0:T(8,128)S(1)}, f32[2,384,128]{1,2,0:T(8,128)S(1)}, u32[]{:S(2)}, u32[]{:S(2)}) collective-permute-start(f32[2,384,128]{1,2,0:T(8,128)S(1)} %get-tuple-element.66), channel_id=1, source_target_pairs={{4,0},{8,4},{12,8},{5,1},{9,5},{13,9},{6,2},{10,6},{14,10},{7,3},{... | collective-permute-start | bytes 1179656 | tf_op jit(solution)/shard_map/ppermute | solution.py:22
  434.3 136.3 %all-reduce.25.cloned.1.call-start = ((), (), s32[]{:S(2)}) async-start(), calls=%async_computation.5 | async-start | bytes 524288 | tf_op jit(solution)/shard_map/psum | solution.py:161
  501.3 17.7 %collective-permute-start.22 = (f32[2,640,128]{1,2,0:T(8,128)S(1)}, f32[2,640,128]{1,2,0:T(8,128)S(1)}, u32[]{:S(2)}, u32[]{:S(2)}) collective-permute-start(f32[2,640,128]{1,2,0:T(8,128)S(1)} %get-tuple-element.23), channel_id=1, source_target_pairs={{0,4},{4,8},{8,12},{1,5},{5,9},{9,13},{2,6},{6,10},{10,14},{3,7},{... | collective-permute-start | bytes 1966088 | tf_op jit(solution)/shard_map/ppermute | solution.py:19
  504.8 30.3 %collective-permute-start.23 = (f32[2,640,128]{1,2,0:T(8,128)S(1)}, f32[2,640,128]{1,2,0:T(8,128)S(1)}, u32[]{:S(2)}, u32[]{:S(2)}) collective-permute-start(f32[2,640,128]{1,2,0:T(8,128)S(1)} %get-tuple-element.24), channel_id=1, source_target_pairs={{4,0},{8,4},{12,8},{5,1},{9,5},{13,9},{6,2},{10,6},{14,10},{7,3},{... | collective-permute-start | bytes 1966088 | tf_op jit(solution)/shard_map/ppermute | solution.py:22
  536.0 108.2 %all-reduce.27.cloned.1.call-start = ((), (), s32[]{:S(2)}) async-start(), calls=%async_computation.6 | async-start | bytes 1048576 | tf_op jit(solution)/shard_map/psum | solution.py:158
  576.5 12.0 %collective-permute-start.26 = (f32[2,384,128]{1,2,0:T(8,128)S(1)}, f32[2,384,128]{1,2,0:T(8,128)S(1)}, u32[]{:S(2)}, u32[]{:S(2)}) collective-permute-start(f32[2,384,128]{1,2,0:T(8,128)S(1)} %get-tuple-element.63), channel_id=1, source_target_pairs={{0,4},{4,8},{8,12},{1,5},{5,9},{9,13},{2,6},{6,10},{10,14},{3,7},{... | collective-permute-start | bytes 1179656 | tf_op jit(solution)/shard_map/ppermute | solution.py:19
  579.9 19.0 %collective-permute-start.27 = (f32[2,384,128]{1,2,0:T(8,128)S(1)}, f32[2,384,128]{1,2,0:T(8,128)S(1)}, u32[]{:S(2)}, u32[]{:S(2)}) collective-permute-start(f32[2,384,128]{1,2,0:T(8,128)S(1)} %get-tuple-element.64), channel_id=1, source_target_pairs={{4,0},{8,4},{12,8},{5,1},{9,5},{13,9},{6,2},{10,6},{14,10},{7,3},{... | collective-permute-start | bytes 1179656 | tf_op jit(solution)/shard_map/ppermute | solution.py:22
  606.6 137.1 %all-reduce.29.cloned.1.call-start = ((), (), s32[]{:S(2)}) async-start(), calls=%async_computation.7 | async-start | bytes 524288 | tf_op jit(solution)/shard_map/psum | solution.py:161
  674.2 17.7 %collective-permute-start.30 = (f32[2,640,128]{1,2,0:T(8,128)S(1)}, f32[2,640,128]{1,2,0:T(8,128)S(1)}, u32[]{:S(2)}, u32[]{:S(2)}) collective-permute-start(f32[2,640,128]{1,2,0:T(8,128)S(1)} %get-tuple-element.21), channel_id=1, source_target_pairs={{0,4},{4,8},{8,12},{1,5},{5,9},{9,13},{2,6},{6,10},{10,14},{3,7},{... | collective-permute-start | bytes 1966088 | tf_op jit(solution)/shard_map/ppermute | solution.py:19
  677.7 30.3 %collective-permute-start.31 = (f32[2,640,128]{1,2,0:T(8,128)S(1)}, f32[2,640,128]{1,2,0:T(8,128)S(1)}, u32[]{:S(2)}, u32[]{:S(2)}) collective-permute-start(f32[2,640,128]{1,2,0:T(8,128)S(1)} %get-tuple-element.22), channel_id=1, source_target_pairs={{4,0},{8,4},{12,8},{5,1},{9,5},{13,9},{6,2},{10,6},{14,10},{7,3},{... | collective-permute-start | bytes 1966088 | tf_op jit(solution)/shard_map/ppermute | solution.py:22
  (49 other events, 461.3 us)
Sparse Core Ops, SparseCore 0:
  42.6 38.9 all-reduce.14
  147.4 34.5 all-reduce.16
  218.0 37.4 all-reduce.18
  320.7 34.5 all-reduce.20
  434.5 36.3 all-reduce.22
  536.1 34.5 all-reduce.24
  606.7 37.4 all-reduce.26
  709.1 34.5 all-reduce.28
where the time goes:
time: 807 us; the launch traced here: 795 us
  waiting for transfers between devices  479 us (59%)
  local copies, waits for them, and re-layouts  90.8 us (11%)
  blocking collectives  80.8 us (10%)
  starting transfers between devices  62.2 us (8%)
  other arithmetic  40.6 us (5%)
  between operations  26.1 us (3%)
  matrix products  15.6 us (2%)
    psum x4, waiting for transfers between devices, mode_total(): return lax.psum(partial_value, 'ma')  148 us
    psum x4, waiting for transfers between devices, combine(): summed = lax.psum(folded, 'ma')  139 us
    ppermute x16, waiting for transfers between devices, padded_2(): lax.ppermute(lax.slice_in_dim(block, 0, width, axis=dim), axis, backward)  118 us
    psum x2, blocking collectives, shards(): norm_now = lax.psum(local_sum(residual, residual), ('gx', 'gy', 'ma'))  80.8 us
    ppermute x16, waiting for transfers between devices, padded_2(): lax.ppermute(lax.slice_in_dim(block, block.shape[dim] - width, None, axis...  74.3 us
    dynamic_update_slice x8, local copies, waits for them, and re-layouts, project(): lax.dynamic_update_slice(extended, lax.dynamic_slice(extended, corner, (2...  61.6 us
    ppermute x16, starting transfers between devices, padded_2(): lax.ppermute(lax.slice_in_dim(block, block.shape[dim] - width, None, axis...  40.8 us
    ppermute x16, starting transfers between devices, padded_2(): lax.ppermute(lax.slice_in_dim(block, 0, width, axis=dim), axis, backward)  20.8 us
  transfers between devices with their start and end apart: 40, of which 35 were waited for; matrix products, arithmetic and copies ran while one was open for 1% of the time, Pallas kernels for 0%

commit v1 on v0

v1 whole, which is shorter than its diff:
```python
import math

import jax
import jax.numpy as jnp
import numpy as np
from jax import lax
from jax.sharding import PartitionSpec as P

OUTER = 2
DAMPING = 1.0


def dft_tables(patch_width):
    ladder = np.arange(patch_width)
    angles = (ladder[:, None] * ladder[None, :] % patch_width) * (2.0 * math.pi / patch_width)
    factor = 1.0 / math.sqrt(patch_width)
    real_part = np.cos(angles) * factor
    imag_part = -np.sin(angles) * factor
    table_one = np.block([[real_part, -imag_part], [imag_part, real_part]])
    table_two = np.block([[real_part, imag_part], [-imag_part, real_part]])
    return jnp.asarray(table_one, jnp.bfloat16), jnp.asarray(table_two, jnp.bfloat16)


def shift_pair(low_part, high_part, axis):
    count = lax.axis_size(axis)
    forward = [(i, i + 1) for i in range(count - 1)]
    backward = [(target, source) for source, target in forward]
    return lax.ppermute(high_part, axis, forward), lax.ppermute(low_part, axis, backward)


def widen(block, axis, dim, width):
    size = block.shape[dim]
    low, high = shift_pair(
        lax.slice_in_dim(block, 0, width, axis=dim),
        lax.slice_in_dim(block, size - width, None, axis=dim),
        axis,
    )
    return jnp.concatenate([low, block, high], axis=dim)


def fold(block, axis, dim, width):
    size = block.shape[dim]
    low, high = shift_pair(
        lax.slice_in_dim(block, 0, width, axis=dim),
        lax.slice_in_dim(block, size - width, None, axis=dim),
        axis,
    )
    middle = lax.slice_in_dim(block, width, size - width, axis=dim)
    pads = [(0, 0)] * 3
    pads[dim] = (0, size - 3 * width)
    first = jnp.pad(low, pads)
    pads[dim] = (size - 3 * width, 0)
    return middle + first + jnp.pad(high, pads)


def shards(object_field, probe_shard, measured, positions, slot_counts):
    patch = probe_shard.shape[-1]
    rim = patch // 2
    rows, cols = object_field.shape[1:]
    slots = measured.shape[2]
    share = patch // lax.axis_size("ma")
    first = lax.axis_index("ma") * share
    table_one, table_two = dft_tables(patch)
    left_one = lax.dynamic_slice_in_dim(table_one.reshape(2, patch, 2, patch), first, share, 1)
    right_two = table_two.reshape(2, patch, 2 * patch)
    left_two = lax.dynamic_slice_in_dim(table_two.reshape(2, patch, 2, patch), first, share, 3)
    targets = lax.dynamic_slice_in_dim(measured[0, 0], first, share, 1)
    centres = positions[0, 0]
    live = (jnp.arange(slots, dtype=jnp.int32) < slot_counts[0, 0]).astype(jnp.float32)
    live = live[:, None, None]
    anchor = jnp.zeros((), jnp.int32)
    probes = lax.all_gather(probe_shard, "ma", axis=0, tiled=True)
    modes = probes.shape[0]
    probe_real, probe_imag = probes[None, :, 0], probes[None, :, 1]

    def spectra_of(tile):
        padded = widen(widen(tile, "gy", 2, rim), "gx", 1, rim)
        windows = jnp.stack(
            [
                lax.dynamic_slice(padded, (anchor, centres[s, 0], centres[s, 1]), (2, patch, patch))
                for s in range(slots)
            ]
        )
        real, imag = windows[:, None, 0], windows[:, None, 1]
        waves = jnp.stack(
            [probe_real * real - probe_imag * imag, probe_real * imag + probe_imag * real], 2
        ).astype(jnp.bfloat16)
        halfway = jnp.einsum(
            "pqci,smcik->smpqk", left_one, waves, preferred_element_type=jnp.float32
        ).astype(jnp.bfloat16)
        return jnp.einsum(
            "smcik,ckl->smil", halfway, right_two, preferred_element_type=jnp.float32
        )

    def mode_sum(first_spectra, second_spectra):
        product = first_spectra * second_spectra
        return jnp.sum(product[..., :patch] + product[..., patch:], axis=1)

    def project(weights, spectra):
        doubled = jnp.concatenate([weights, weights], -1)[:, None]
        scaled = (2.0 * spectra * doubled).astype(jnp.bfloat16)
        turned = jnp.einsum(
            "smik,kl->smil", scaled, table_one, preferred_element_type=jnp.float32
        ).astype(jnp.bfloat16)
        back = jnp.einsum(
            "pqci,smicl->smpql",
            left_two,
            turned.reshape(slots, modes, share, 2, patch),
            preferred_element_type=jnp.float32,
        )
        real = jnp.sum(probe_real * back[:, :, 0] + probe_imag * back[:, :, 1], axis=1)
        imag = jnp.sum(probe_real * back[:, :, 1] - probe_imag * back[:, :, 0], axis=1)
        pieces = jnp.stack([real, imag], 1)
        canvas = jnp.zeros((2, rows + patch, cols + patch), jnp.float32)
        room = jnp.pad(pieces, ((0, 0), (0, 0), (rows, rows), (cols, cols)))
        for s in range(slots):
            canvas = canvas + lax.dynamic_slice(
                room[s], (anchor, rows - centres[s, 0], cols - centres[s, 1]), canvas.shape
            )
        return lax.psum(fold(fold(canvas, "gx", 1, rim), "gy", 2, rim), "ma")

    current = object_field
    spectra = spectra_of(current)
    for outer_step in range(OUTER):
        misfit = live * (mode_sum(spectra, spectra) - targets)
        direction = -project(misfit, spectra)
        moved = spectra_of(direction)
        change = 2.0 * live * mode_sum(spectra, moved)
        sums = jnp.stack(
            [jnp.sum(direction * direction) / lax.axis_size("ma"), jnp.sum(change * change)]
        )
        sums = lax.psum(sums, ("gx", "gy", "ma"))
        step_size = sums[0] / (DAMPING * sums[0] + sums[1])
        current = current + step_size * direction
        if outer_step + 1 < OUTER:
            spectra = spectra + step_size * moved
    return current


def solution(mesh):
    return jax.shard_map(
        shards,
        mesh=mesh,
        in_specs=(
            P(None, "gx", "gy"),
            P("ma", None, None, None),
            P("gx", "gy", None, None, None),
            P("gx", "gy", None, None),
            P("gx", "gy"),
        ),
        out_specs=P(None, "gx", "gy"),
        check_vma=False,
    )
```

time: 807 us -> 403 us (0.50); the launches traced: 795 us -> 402 us
  waiting for transfers between devices: 479 us -> 162 us
  local copies, waits for them, and re-layouts: 90.8 us -> 22.3 us
  starting transfers between devices: 62.2 us -> 39.5 us
  matrix products: 15.6 us -> 24.5 us
    psum x8 -> x2, waiting for transfers between devices: 286 us -> 68.5 us  [project(): return lax.psum(fold(fold(canvas, 'gx', 1, rim), 'gy', 2, rim), 'ma')]
    ppermute x32 -> x20, waiting for transfers between devices: 193 us -> 37.9 us  [the longest x10 30.2 us: shift_pair(): lax.ppermute(low_part, axis, backward)]
    dynamic_update_slice x8 -> x0, local copies, waits for them, and re-layouts: 61.6 us -> none  [project(): lax.dynamic_update_slice(extended, lax.dynamic_slice(extended, corner, (2...]
    all_gather x0 -> x1, waiting for transfers between devices: none -> 54.5 us  [shards(): probes = lax.all_gather(probe_shard, 'ma', axis=0, tiled=True)]
    ppermute x32 -> x20, starting transfers between devices: 61.7 us -> 39.4 us  [the longest x10 26.1 us: shift_pair(): lax.ppermute(high_part, axis, forward)]
    another operation x4 -> x7, other arithmetic: 1.16 us -> 14.5 us
    dot_general x16 -> x7, matrix products: 15.6 us -> 24.5 us  [the longest x3 17.3 us: spectra_of(): jnp.einsum('smcik,ckl->smil', halfway, right_two, preferred_element_type=...]
  transfers between devices with their start and end apart: 40 -> 23, of which waited for: 35 -> 19; matrix products, arithmetic and copies ran while one was open for 1% -> 1% of each run, Pallas kernels for 0% -> 0%
where the time goes in v1:
time: 403 us; the launch traced here: 402 us
  waiting for transfers between devices  162 us (40%)
  blocking collectives  79.6 us (20%)
  other arithmetic  42 us (10%)
  starting transfers between devices  39.5 us (10%)
  between operations  31.9 us (8%)
  matrix products  24.5 us (6%)
  local copies, waits for them, and re-layouts  22.3 us (6%)
    psum x2, blocking collectives, shards(): sums = lax.psum(sums, ('gx', 'gy', 'ma'))  79.6 us
    psum x2, waiting for transfers between devices, project(): return lax.psum(fold(fold(canvas, 'gx', 1, rim), 'gy', 2, rim), 'ma')  68.5 us
    all_gather x1, waiting for transfers between devices, shards(): probes = lax.all_gather(probe_shard, 'ma', axis=0, tiled=True)  54.5 us
    ppermute x10, waiting for transfers between devices, shift_pair(): lax.ppermute(low_part, axis, backward)  30.2 us
    ppermute x10, starting transfers between devices, shift_pair(): lax.ppermute(high_part, axis, forward)  26.1 us
    dot_general x3, matrix products, spectra_of(): jnp.einsum('smcik,ckl->smil', halfway, right_two, preferred_element_type=...  17.3 us
    ppermute x10, starting transfers between devices, shift_pair(): lax.ppermute(low_part, axis, backward)  13.3 us
    another operation x3, other arithmetic  11.4 us
  transfers between devices with their start and end apart: 23, of which 19 were waited for; matrix products, arithmetic and copies ran while one was open for 1% of the time, Pallas kernels for 0%

profile of v1, /device:TPU:0, one launch (start us, length us, event | category | flops | bytes accessed | tf_op | source)
XLA Modules:
  0.0 401.5 jit_solution(1194735594641044020)
XLA Ops:
  8.3 4.9 %collective-permute-start = (f32[2,128,128]{2,1,0:T(8,128)S(1)}, f32[2,128,128]{2,1,0:T(8,128)S(1)}, u32[]{:S(2)}, u32[]{:S(2)}) collective-permute-start(f32[2,128,128]{2,1,0:T(8,128)S(1)} %get-tuple-element.52), channel_id=1, source_target_pairs={{0,4},{4,8},{8,12},{1,5},{5,9},{9,13},{2,6},{6,10},{10,14},{3,7},{... | collective-permute-start | bytes 393224 | tf_op jit(solution)/shard_map/ppermute | solution.py:28
  16.9 3.8 collective-permute-done.1
  37.9 54.5 %all-gather.2.cloned.1.call-done = f32[8,2,256,256]{3,2,1,0:T(8,128)} async-done(((f32[2,2,256,256]{3,2,1,0:T(8,128)}), f32[8,2,256,256]{3,2,1,0:T(8,128)}) %all-gather.2.cloned.1.call-update) | async-done | bytes 4194320 | tf_op jit(solution)/shard_map/all_gather | solution.py:72
  92.4 4.0 slice_bitcast_fusion.5
  98.2 2.9 copy.45
  101.1 4.8 %subtract_convert_fusion.2 = (bf16[2,8,1,256,256]{4,3,2,1,0:T(8,128)(2,1)}, bf16[2,8,1,256,256]{4,3,2,1,0:T(8,128)(2,1)}) fusion(f32[2,256,256]{2,1,0:T(8,128)S(1)} %get-tuple-element.38, f32[8,256,256]{2,1,0:T(8,128)} %get-tuple-element.22, f32[2,256,256]{2,1,0:T(8,128)S(1)} %get-tuple-element.37, f32[8,256,256]{2,1,0:T(8,128)S(1)} %get-tuple-element.21), kind=kLoop, calls=%fused_computation.41 | loop fusion | flops 8388608 | bytes 9437184 | tf_op jit(solution)/shard_map/convert.4
  105.8 5.6 %bitcast_multiply_fusion.4 = (f32[2,8,64,512]{3,2,1,0:T(8,128)}, f32[2,8,64,512,1]{3,2,4,1,0:T(8,128)}) fusion(bf16[2,256,512,1,1]{2,1,0,4,3:T(8,128)(2,1)} %constant.64, bf16[2,8,1,256,256]{4,3,2,1,0:T(8,128)(2,1)} %get-tuple-element.20, bf16[2,8,1,256,256]{4,3,2,1,0:T(8,128)(2,1)} %get-tuple-element.19, bf16[2,256,2,256]{3,1,2,0:T(8,128)(2,1)} %constant.61, ...), kind=kOutput, calls=%fused_computation.53 | convolution fusion | flops 1083179008 | bytes 9043972 | tf_op jit(solution)/shard_map/smcik,ckl->smil/dot_general | solution.py:91
  129.6 3.4 collective-permute-start.6
  136.0 4.7 %collective-permute-done.7 = f32[2,128,128]{1,2,0:T(8,128)S(1)} collective-permute-done((f32[2,128,128]{1,2,0:T(8,128)S(1)}, f32[2,128,128]{1,2,0:T(8,128)S(1)}, u32[]{:S(2)}, u32[]{:S(2)}) %collective-permute-start.7) | collective-permute-done | bytes 131104 | tf_op jit(solution)/shard_map/ppermute | solution.py:28
  141.5 33.7 %all-reduce.9.cloned.1.call-done = f32[2,128,256]{1,2,0:T(8,128)} async-done(((f32[2,128,256]{1,2,0:T(8,128)}), f32[2,128,256]{1,2,0:T(8,128)}) %all-reduce.9.cloned.1.call-update) | async-done | bytes 262160 | tf_op jit(solution)/shard_map/psum | solution.py:120
  177.0 3.4 collective-permute-start.8
  182.9 4.4 %collective-permute-done.9 = f32[2,128,128]{1,2,0:T(8,128)S(1)} collective-permute-done((f32[2,128,128]{1,2,0:T(8,128)S(1)}, f32[2,128,128]{1,2,0:T(8,128)S(1)}, u32[]{:S(2)}, u32[]{:S(2)}) %collective-permute-start.9) | collective-permute-done | bytes 131104 | tf_op jit(solution)/shard_map/ppermute | solution.py:28
  197.8 3.4 subtract_convert_fusion.1
  201.2 6.2 %bitcast_multiply_fusion.2 = (f32[2,8,64,512]{3,2,1,0:T(8,128)}, f32[2,8,64,512,1]{3,2,4,1,0:T(8,128)}) fusion(f32[2,8,64,512,1]{3,2,4,1,0:T(8,128)} %get-tuple-element.62, bf16[2,256,512,1,1]{2,1,0,4,3:T(8,128)(2,1)S(1)} %copy-done.13, bf16[2,8,1,256,256]{4,3,2,1,0:T(8,128)(2,1)} %get-tuple-element.18, bf16[2,8,1,256,256]{4,3,2,1,0:T(8,128)(2,1)} %get-tuple-element.17, ...), kind=kOutput, calls=%fused_computation.49 | convolution fusion | flops 1083179008 | bytes 11141124 | tf_op jit(solution)/shard_map/smcik,ckl->smil/dot_general | solution.py:91
  210.4 39.8 %psum.29 = f32[2]{0:T(128)S(1)} all-reduce(f32[2]{0:T(128)S(1)} %pad_maximum_fusion.8), channel_id=1, replica_groups=mesh['gx'=2,'gy'=4,'ma'=4] {'gx','gy','ma'}, use_global_device_ids=true, to_apply=%region_7.8 | all-reduce | flops 2 | bytes 16 | tf_op jit(solution)/shard_map/psum | solution.py:132
  252.5 3.0 fusion.72
  269.8 4.2 %collective-permute-start.14 = (f32[2,128,128]{1,2,0:T(8,128)S(1)}, f32[2,128,128]{1,2,0:T(8,128)S(1)}, u32[]{:S(2)}, u32[]{:S(2)}) collective-permute-start(f32[2,128,128]{1,2,0:T(8,128)S(1)} %get-tuple-element.39), channel_id=1, source_target_pairs={{0,4},{4,8},{8,12},{1,5},{5,9},{9,13},{2,6},{6,10},{10,14},{3,7},{... | collective-permute-start | bytes 393224 | tf_op jit(solution)/shard_map/ppermute | solution.py:28
  277.0 4.7 %collective-permute-done.15 = f32[2,128,128]{1,2,0:T(8,128)S(1)} collective-permute-done((f32[2,128,128]{1,2,0:T(8,128)S(1)}, f32[2,128,128]{1,2,0:T(8,128)S(1)}, u32[]{:S(2)}, u32[]{:S(2)}) %collective-permute-start.15) | collective-permute-done | bytes 131104 | tf_op jit(solution)/shard_map/ppermute | solution.py:28
  282.5 34.8 %all-reduce.11.cloned.1.call-done = f32[2,128,256]{1,2,0:T(8,128)} async-done(((f32[2,128,256]{1,2,0:T(8,128)}), f32[2,128,256]{1,2,0:T(8,128)}) %all-reduce.11.cloned.1.call-update) | async-done | bytes 262160 | tf_op jit(solution)/shard_map/psum | solution.py:120
  318.9 3.4 collective-permute-start.16
  324.8 4.4 %collective-permute-done.17 = f32[2,128,128]{1,2,0:T(8,128)S(1)} collective-permute-done((f32[2,128,128]{1,2,0:T(8,128)S(1)}, f32[2,128,128]{1,2,0:T(8,128)S(1)}, u32[]{:S(2)}, u32[]{:S(2)}) %collective-permute-start.17) | collective-permute-done | bytes 131104 | tf_op jit(solution)/shard_map/ppermute | solution.py:28
  339.6 3.3 subtract_convert_fusion
  342.9 5.5 %bitcast_multiply_fusion = f32[2,8,64,512]{3,2,1,0:T(8,128)} fusion(f32[2,8,64,512]{3,2,1,0:T(8,128)} %copy-done.7, bf16[2,256,512,1,1]{2,1,0,4,3:T(8,128)(2,1)S(1)} %copy-done.14, bf16[2,8,1,256,256]{4,3,2,1,0:T(8,128)(2,1)} %get-tuple-element.16, bf16[2,8,1,256,256]{4,3,2,1,0:T(8,128)(2,1)} %get-tuple-element.15, bf16[2,256,2,256]{3,1,2,0:T(8,128)(2,1)} %constant.61, ...), kind=kOutput, calls=%fused_computation.46 | convolution fusion | flops 1083179008 | bytes 9043972 | tf_op jit(solution)/shard_map/smcik,ckl->smil/dot_general | solution.py:91
  351.8 39.8 %psum.31 = f32[2]{0:T(128)S(1)} all-reduce(f32[2]{0:T(128)S(1)} %pad_maximum_fusion.9), channel_id=1, replica_groups=mesh['gx'=2,'gy'=4,'ma'=4] {'gx','gy','ma'}, use_global_device_ids=true, to_apply=%region_15.16 | all-reduce | flops 2 | bytes 16 | tf_op jit(solution)/shard_map/psum | solution.py:132
  (137 shorter events, 87.2 us)
Async XLA Ops:
  6.5 85.9 %all-gather.2.cloned.1.call-start = ((), (), s32[]{:S(2)}) async-start(), calls=%async_computation | async-start | bytes 5242880 | tf_op jit(solution)/shard_map/all_gather | solution.py:72
  7.3 168.0 %all-reduce.9.cloned.1.call-start = ((), (), s32[]{:S(2)}) async-start(), calls=%async_computation.1 | async-start | bytes 524288 | tf_op jit(solution)/shard_map/psum | solution.py:120
  8.3 7.6 %collective-permute-start = (f32[2,128,128]{2,1,0:T(8,128)S(1)}, f32[2,128,128]{2,1,0:T(8,128)S(1)}, u32[]{:S(2)}, u32[]{:S(2)}) collective-permute-start(f32[2,128,128]{2,1,0:T(8,128)S(1)} %get-tuple-element.52), channel_id=1, source_target_pairs={{0,4},{4,8},{8,12},{1,5},{5,9},{9,13},{2,6},{6,10},{10,14},{3,7},{... | collective-permute-start | bytes 393224 | tf_op jit(solution)/shard_map/ppermute | solution.py:28
  13.2 7.5 %collective-permute-start.1 = (f32[2,128,128]{2,1,0:T(8,128)S(1)}, f32[2,128,128]{2,1,0:T(8,128)S(1)}, u32[]{:S(2)}, u32[]{:S(2)}) collective-permute-start(f32[2,128,128]{2,1,0:T(8,128)S(1)} %get-tuple-element.51), channel_id=1, source_target_pairs={{4,0},{8,4},{12,8},{5,1},{9,5},{13,9},{6,2},{10,6},{14,10},{7,3},{... | collective-permute-start | bytes 393224 | tf_op jit(solution)/shard_map/ppermute | solution.py:28
  20.7 16.6 %collective-permute-start.2 = (f32[2,128,512]{2,1,0:T(8,128)S(1)}, f32[2,128,512]{2,1,0:T(8,128)S(1)}, u32[]{:S(2)}, u32[]{:S(2)}) collective-permute-start(f32[2,128,512]{2,1,0:T(8,128)S(1)} %constant_dynamic-update-slice_fusion), channel_id=1, source_target_pairs={{0,16},{1,17},{2,18},{3,19},{4,20},{5,21},{6,22},{7,23},{8,24},{9,... | collective-permute-start | bytes 1572872 | tf_op jit(solution)/shard_map/ppermute | solution.py:28
  22.0 15.2 %collective-permute-start.3 = (f32[2,128,512]{2,1,0:T(8,128)S(1)}, f32[2,128,512]{2,1,0:T(8,128)S(1)}, u32[]{:S(2)}, u32[]{:S(2)}) collective-permute-start(f32[2,128,512]{2,1,0:T(8,128)S(1)} %constant_dynamic-update-slice_fusion), channel_id=1, source_target_pairs={{16,0},{17,1},{18,2},{19,3},{20,4},{21,5},{22,6},{23,7},{24,8},{25... | collective-permute-start | bytes 1572872 | tf_op jit(solution)/shard_map/ppermute | solution.py:28
  124.0 3.1 collective-permute-start.4
  125.6 3.8 collective-permute-start.5
  129.6 6.4 %collective-permute-start.6 = (f32[2,128,128]{1,2,0:T(8,128)S(1)}, f32[2,128,128]{1,2,0:T(8,128)S(1)}, u32[]{:S(2)}, u32[]{:S(2)}) collective-permute-start(f32[2,128,128]{1,2,0:T(8,128)S(1)} %get-tuple-element.41), channel_id=1, source_target_pairs={{0,4},{4,8},{8,12},{1,5},{5,9},{9,13},{2,6},{6,10},{10,14},{3,7},{... | collective-permute-start | bytes 393224 | tf_op jit(solution)/shard_map/ppermute | solution.py:28
  132.9 7.8 %collective-permute-start.7 = (f32[2,128,128]{1,2,0:T(8,128)S(1)}, f32[2,128,128]{1,2,0:T(8,128)S(1)}, u32[]{:S(2)}, u32[]{:S(2)}) collective-permute-start(f32[2,128,128]{1,2,0:T(8,128)S(1)} %get-tuple-element.42), channel_id=1, source_target_pairs={{4,0},{8,4},{12,8},{5,1},{9,5},{13,9},{6,2},{10,6},{14,10},{7,3},{... | collective-permute-start | bytes 393224 | tf_op jit(solution)/shard_map/ppermute | solution.py:28
  141.5 175.8 %all-reduce.11.cloned.1.call-start = ((), (), s32[]{:S(2)}) async-start(), calls=%async_computation.2 | async-start | bytes 524288 | tf_op jit(solution)/shard_map/psum | solution.py:120
  177.0 5.9 %collective-permute-start.8 = (f32[2,128,128]{1,2,0:T(8,128)S(1)}, f32[2,128,128]{1,2,0:T(8,128)S(1)}, u32[]{:S(2)}, u32[]{:S(2)}) collective-permute-start(f32[2,128,128]{1,2,0:T(8,128)S(1)} %get-tuple-element.49), channel_id=1, source_target_pairs={{0,4},{4,8},{8,12},{1,5},{5,9},{9,13},{2,6},{6,10},{10,14},{3,7},{... | collective-permute-start | bytes 393224 | tf_op jit(solution)/shard_map/ppermute | solution.py:28
  180.4 6.9 %collective-permute-start.9 = (f32[2,128,128]{1,2,0:T(8,128)S(1)}, f32[2,128,128]{1,2,0:T(8,128)S(1)}, u32[]{:S(2)}, u32[]{:S(2)}) collective-permute-start(f32[2,128,128]{1,2,0:T(8,128)S(1)} %get-tuple-element.50), channel_id=1, source_target_pairs={{4,0},{8,4},{12,8},{5,1},{9,5},{13,9},{6,2},{10,6},{14,10},{7,3},{... | collective-permute-start | bytes 393224 | tf_op jit(solution)/shard_map/ppermute | solution.py:28
  187.9 3.5 collective-permute-start.10
  189.3 3.9 collective-permute-start.11
  264.5 2.8 collective-permute-start.12
  265.8 3.8 collective-permute-start.13
  269.8 7.2 %collective-permute-start.14 = (f32[2,128,128]{1,2,0:T(8,128)S(1)}, f32[2,128,128]{1,2,0:T(8,128)S(1)}, u32[]{:S(2)}, u32[]{:S(2)}) collective-permute-start(f32[2,128,128]{1,2,0:T(8,128)S(1)} %get-tuple-element.39), channel_id=1, source_target_pairs={{0,4},{4,8},{8,12},{1,5},{5,9},{9,13},{2,6},{6,10},{10,14},{3,7},{... | collective-permute-start | bytes 393224 | tf_op jit(solution)/shard_map/ppermute | solution.py:28
  274.0 7.8 %collective-permute-start.15 = (f32[2,128,128]{1,2,0:T(8,128)S(1)}, f32[2,128,128]{1,2,0:T(8,128)S(1)}, u32[]{:S(2)}, u32[]{:S(2)}) collective-permute-start(f32[2,128,128]{1,2,0:T(8,128)S(1)} %get-tuple-element.40), channel_id=1, source_target_pairs={{4,0},{8,4},{12,8},{5,1},{9,5},{13,9},{6,2},{10,6},{14,10},{7,3},{... | collective-permute-start | bytes 393224 | tf_op jit(solution)/shard_map/ppermute | solution.py:28
  318.9 5.9 %collective-permute-start.16 = (f32[2,128,128]{1,2,0:T(8,128)S(1)}, f32[2,128,128]{1,2,0:T(8,128)S(1)}, u32[]{:S(2)}, u32[]{:S(2)}) collective-permute-start(f32[2,128,128]{1,2,0:T(8,128)S(1)} %get-tuple-element.45), channel_id=1, source_target_pairs={{0,4},{4,8},{8,12},{1,5},{5,9},{9,13},{2,6},{6,10},{10,14},{3,7},{... | collective-permute-start | bytes 393224 | tf_op jit(solution)/shard_map/ppermute | solution.py:28
  322.3 6.9 %collective-permute-start.17 = (f32[2,128,128]{1,2,0:T(8,128)S(1)}, f32[2,128,128]{1,2,0:T(8,128)S(1)}, u32[]{:S(2)}, u32[]{:S(2)}) collective-permute-start(f32[2,128,128]{1,2,0:T(8,128)S(1)} %get-tuple-element.46), channel_id=1, source_target_pairs={{4,0},{8,4},{12,8},{5,1},{9,5},{13,9},{6,2},{10,6},{14,10},{7,3},{... | collective-permute-start | bytes 393224 | tf_op jit(solution)/shard_map/ppermute | solution.py:28
  329.9 3.4 collective-permute-start.18
  331.2 3.9 collective-permute-start.19
  348.5 45.6 %copy-start.12 = (f32[2,128,256]{1,2,0:T(8,128)S(1)}, f32[2,128,256]{1,2,0:T(8,128)}, u32[]{:S(2)}) copy-start(f32[2,128,256]{1,2,0:T(8,128)} %all-reduce.11.cloned.1.call-done) | copy-start | bytes 786436
  (17 other events, 96.5 us)
Sparse Core Ops, SparseCore 0:
  8.9 83.4 all-gather.1
  141.6 33.6 all-reduce.8
  282.6 34.6 all-reduce.10

commit v2 on v1

--- a/solution.py
+++ b/solution.py
@@ -1,9 +1,12 @@
+import functools
 import math
 
 import jax
 import jax.numpy as jnp
 import numpy as np
 from jax import lax
+from jax.experimental import pallas as pl
+from jax.experimental.pallas import tpu as pltpu
 from jax.sharding import PartitionSpec as P
 
 OUTER = 2
@@ -21,36 +24,332 @@
     return jnp.asarray(table_one, jnp.bfloat16), jnp.asarray(table_two, jnp.bfloat16)
 
 
-def shift_pair(low_part, high_part, axis):
-    count = lax.axis_size(axis)
-    forward = [(i, i + 1) for i in range(count - 1)]
-    backward = [(target, source) for source, target in forward]
-    return lax.ppermute(high_part, axis, forward), lax.ppermute(low_part, axis, backward)
-
-
-def widen(block, axis, dim, width):
-    size = block.shape[dim]
-    low, high = shift_pair(
-        lax.slice_in_dim(block, 0, width, axis=dim),
-        lax.slice_in_dim(block, size - width, None, axis=dim),
-        axis,
-    )
-    return jnp.concatenate([low, block, high], axis=dim)
-
-
-def fold(block, axis, dim, width):
-    size = block.shape[dim]
-    low, high = shift_pair(
-        lax.slice_in_dim(block, 0, width, axis=dim),
-        lax.slice_in_dim(block, size - width, None, axis=dim),
-        axis,
-    )
-    middle = lax.slice_in_dim(block, width, size - width, axis=dim)
-    pads = [(0, 0)] * 3
-    pads[dim] = (0, size - 3 * width)
-    first = jnp.pad(low, pads)
-    pads[dim] = (size - 3 * width, 0)
-    return middle + first + jnp.pad(high, pads)
+MESH = pl.DeviceIdType.MESH
+VMEM = pl.BlockSpec(memory_space=pltpu.VMEM)
+
+
+def remote(source, target, sends, recvs, slot, axis, index):
+    return pltpu.make_async_remote_copy(
+        src_ref=source,
+        dst_ref=target,
+        send_sem=sends.at[slot],
+        recv_sem=recvs.at[slot],
+        device_id={axis: index},
+        device_id_type=MESH,
+    )
+
+
+def greet(lines, groups):
+    barrier = pltpu.get_barrier_semaphore()
+
+    def call(axis, index):
+        pl.semaphore_signal(barrier, inc=1, device_id={axis: index}, device_id_type=MESH)
+
+    peers = jnp.int32(0)
+    for axis in lines:
+        me, count = lax.axis_index(axis), lax.axis_size(axis)
+        pl.when(me > 0)(functools.partial(call, axis, me - 1))
+        pl.when(me < count - 1)(functools.partial(call, axis, me + 1))
+        peers = peers + jnp.minimum(me, 1) + jnp.minimum(count - 1 - me, 1)
+    for axis in groups:
+        me, count = lax.axis_index(axis), lax.axis_size(axis)
+        for step in range(1, count):
+            call(axis, lax.rem(me + step, count))
+        peers = peers + (count - 1)
+    pl.semaphore_wait(barrier, peers)
+
+
+def swap_start(axis, low_from, high_from, low_to, high_to, sends, recvs, slot):
+    me, count = lax.axis_index(axis), lax.axis_size(axis)
+
+    @pl.when(me > 0)
+    def _():
+        remote(low_from, high_to, sends, recvs, slot, axis, me - 1).start()
+
+    @pl.when(me < count - 1)
+    def _():
+        remote(high_from, low_to, sends, recvs, slot + 1, axis, me + 1).start()
+
+
+def swap_wait(axis, low_from, high_from, low_to, high_to, sends, recvs, slot):
+    me, count = lax.axis_index(axis), lax.axis_size(axis)
+
+    @pl.when(me > 0)
+    def _():
+        remote(low_from, high_to, sends, recvs, slot, axis, me - 1).wait_send()
+        remote(high_from, low_to, sends, recvs, slot + 1, axis, me - 1).wait_recv()
+
+    @pl.when(me == 0)
+    def _():
+        low_to[...] = jnp.zeros(low_to.shape, low_to.dtype)
+
+    @pl.when(me < count - 1)
+    def _():
+        remote(high_from, low_to, sends, recvs, slot + 1, axis, me + 1).wait_send()
+        remote(low_from, high_to, sends, recvs, slot, axis, me + 1).wait_recv()
+
+    @pl.when(me == count - 1)
+    def _():
+        high_to[...] = jnp.zeros(high_to.shape, high_to.dtype)
+
+
+def swap(*arguments):
+    swap_start(*arguments)
+    swap_wait(*arguments)
+
+
+def column_halo(pad, rim, rows, cols, sends, recvs, slot):
+    body = pl.ds(rim, rows)
+    return (
+        "gy",
+        pad.at[:, body, pl.ds(rim, rim)],
+        pad.at[:, body, pl.ds(cols, rim)],
+        pad.at[:, body, pl.ds(0, rim)],
+        pad.at[:, body, pl.ds(rim + cols, rim)],
+        sends,
+        recvs,
+        slot,
+    )
+
+
+def row_halo(pad, rim, rows, cols, sends, recvs, slot):
+    return (
+        "gx",
+        pad.at[:, pl.ds(rim, rim)],
+        pad.at[:, pl.ds(rows, rim)],
+        pad.at[:, pl.ds(0, rim)],
+        pad.at[:, pl.ds(rim + rows, rim)],
+        sends,
+        recvs,
+        slot,
+    )
+
+
+def gather_kernel(rim, probe_ref, tile_ref, probes_ref, padded_ref, all_probes, pad, sends, recvs):
+    rows, cols = tile_ref.shape[1:]
+    own = probe_ref.shape[0]
+    half = probe_ref.shape[2] // 2
+    me, count = lax.axis_index("ma"), lax.axis_size("ma")
+    cell = lax.axis_index("gx")
+    paired = lax.axis_size("gx") % 2 == 0
+    greet(("gx", "gy"), ("ma",))
+    part = lax.rem(cell, 2)
+    mate = cell + 1 - 2 * part
+    halves = pl.ds(pl.multiple_of(part * half, half), half) if paired else pl.ds(0, 2 * half)
+
+    def block(owner):
+        return all_probes.at[pl.ds(owner * own, own), :, halves]
+
+    def out_copy(step):
+        to = lax.rem(me + step, count)
+        return remote(
+            probe_ref.at[:, :, halves], block(me), sends, recvs, 3 + step, "ma", to
+        )
+
+    for step in range(1, count):
+        out_copy(step).start()
+    pad[:, pl.ds(rim, rows), pl.ds(rim, cols)] = tile_ref[...]
+    swap(*column_halo(pad, rim, rows, cols, sends, recvs, 0))
+    swap(*row_halo(pad, rim, rows, cols, sends, recvs, 2 + count + 1))
+    padded_ref[...] = pad[...]
+    all_probes[pl.ds(me * own, own)] = probe_ref[...]
+    base = 5 + count
+
+    def pass_on(step):
+        owner = lax.rem(me + count - step, count)
+        return remote(block(owner), block(owner), sends, recvs, base + step, "gx", mate)
+
+    def arrival(step):
+        owner = lax.rem(me + count - step, count)
+        return remote(
+            probe_ref.at[:, :, halves], block(owner), sends, recvs, 3 + step, "ma", owner
+        )
+
+    for step in range(1, count):
+        arrival(step).wait_recv()
+        if paired:
+            pass_on(step).start()
+    for step in range(1, count):
+        out_copy(step).wait_send()
+        if paired:
+            pass_on(step).wait_send()
+            pass_on(step).wait_recv()
+    probes_ref[...] = all_probes[...]
+
+
+def gather(probe_shard, tile):
+    own, _, patch, _ = probe_shard.shape
+    count = lax.axis_size("ma")
+    rows, cols = tile.shape[1:]
+    probes = jax.ShapeDtypeStruct((own * count, 2, patch, patch), jnp.float32)
+    padded = jax.ShapeDtypeStruct((2, rows + patch, cols + patch), jnp.float32)
+    return pl.pallas_call(
+        functools.partial(gather_kernel, patch // 2),
+        out_shape=(probes, padded),
+        in_specs=[VMEM] * 2,
+        out_specs=(VMEM, VMEM),
+        scratch_shapes=[
+            pltpu.VMEM(probes.shape, jnp.float32),
+            pltpu.VMEM(padded.shape, jnp.float32),
+            pltpu.SemaphoreType.DMA((5 + 2 * count,)),
+            pltpu.SemaphoreType.DMA((5 + 2 * count,)),
+        ],
+        compiler_params=pltpu.CompilerParams(
+            collective_id=0, has_side_effects=True, vmem_limit_bytes=40 << 20
+        ),
+    )(probe_shard, tile)
+
+
+def fold_rows(tile):
+    total = jnp.zeros((8, 128), jnp.float32)
+    for i in range(tile.shape[0] // 8):
+        for j in range(tile.shape[1] // 128):
+            total = total + tile[8 * i : 8 * i + 8, 128 * j : 128 * j + 128]
+    return total
+
+
+def settle_kernel(
+    rim, canvas_ref, padded_ref, norm_ref, gx_in, mid, gy_in, tile, ma_in, pad, sends, recvs
+):
+    rows, cols = tile.shape[1:]
+    me, count = lax.axis_index("ma"), lax.axis_size("ma")
+    share = rows // count
+    greet(("gx", "gy"), ("ma",))
+    swap(
+        "gx",
+        canvas_ref.at[:, pl.ds(0, rim)],
+        canvas_ref.at[:, pl.ds(rim + rows, rim)],
+        gx_in.at[0],
+        gx_in.at[1],
+        sends,
+        recvs,
+        0,
+    )
+    mid[...] = canvas_ref[:, rim : rim + rows]
+    mid[:, :rim] += gx_in[0]
+    mid[:, rows - rim :] += gx_in[1]
+    swap(
+        "gy",
+        mid.at[:, :, pl.ds(0, rim)],
+        mid.at[:, :, pl.ds(rim + cols, rim)],
+        gy_in.at[0],
+        gy_in.at[1],
+        sends,
+        recvs,
+        2,
+    )
+    tile[...] = mid[:, :, rim : rim + cols]
+    tile[:, :, :rim] += gy_in[0]
+    tile[:, :, cols - rim :] += gy_in[1]
+
+    def band(owner, start=0):
+        return pl.ds(pl.multiple_of(start + owner * share, 8), share)
+
+    def scatter(step):
+        to = lax.rem(me + step, count)
+        return remote(
+            tile.at[:, band(to)], ma_in.at[step - 1], sends, recvs, 8 + step, "ma", to
+        )
+
+    for step in range(1, count):
+        scatter(step).start()
+    total = tile[:, band(me)]
+    for step in range(1, count):
+        scatter(step).wait_recv()
+        total = total + ma_in[step - 1]
+    total = -total
+    pad[:, band(me, rim), pl.ds(rim, cols)] = total
+    norm_ref[...] = fold_rows(total[0] * total[0] + total[1] * total[1])
+
+    def spread(step, owner, to):
+        piece = pad.at[:, band(owner, rim), pl.ds(rim, cols)]
+        return remote(piece, piece, sends, recvs, 8 + count + step, "ma", to)
+
+    for step in range(1, count):
+        spread(step, me, lax.rem(me + step, count)).start()
+    for step in range(1, count):
+        owner = lax.rem(me + count - step, count)
+        spread(step, owner, owner).wait_recv()
+    swap(*column_halo(pad, rim, rows, cols, sends, recvs, 4))
+    swap(*row_halo(pad, rim, rows, cols, sends, recvs, 6))
+    for step in range(1, count):
+        to = lax.rem(me + step, count)
+        scatter(step).wait_send()
+        spread(step, me, to).wait_send()
+    padded_ref[...] = pad[...]
+
+
+def settle(canvas, patch):
+    rim = patch // 2
+    rows, cols = canvas.shape[1] - patch, canvas.shape[2] - patch
+    count = lax.axis_size("ma")
+    f32 = jnp.float32
+    return pl.pallas_call(
+        functools.partial(settle_kernel, rim),
+        out_shape=(
+            jax.ShapeDtypeStruct(canvas.shape, f32),
+            jax.ShapeDtypeStruct((8, 128), f32),
+        ),
+        in_specs=[VMEM],
+        out_specs=(VMEM, VMEM),
+        scratch_shapes=[
+            pltpu.VMEM((2, 2, rim, cols + patch), f32),
+            pltpu.VMEM((2, rows, cols + patch), f32),
+            pltpu.VMEM((2, 2, rows, rim), f32),
+            pltpu.VMEM((2, rows, cols), f32),
+            pltpu.VMEM((count, 2, rows // count, cols), f32),
+            pltpu.VMEM(canvas.shape, f32),
+            pltpu.SemaphoreType.DMA((8 + 2 * count,)),
+            pltpu.SemaphoreType.DMA((8 + 2 * count,)),
+        ],
+        compiler_params=pltpu.CompilerParams(
+            collective_id=1, has_side_effects=True, vmem_limit_bytes=40 << 20
+        ),
+    )(canvas)
+
+
+AXES = ("ma", "gy", "gx")
+
+
+def total_kernel(value_ref, out_ref, *scratch):
+    greet((), AXES)
+    stages = len(AXES)
+    for place, axis in enumerate(AXES):
+        held, sends, recvs = scratch[place], scratch[stages + place], scratch[2 * stages + place]
+        me, count = lax.axis_index(axis), lax.axis_size(axis)
+        held[me] = value_ref[...] if place == 0 else value
+        for step in range(1, count):
+            to = lax.rem(me + step, count)
+            pltpu.make_async_remote_copy(
+                held.at[me], held.at[me], sends.at[step], recvs.at[step], {axis: to}, MESH
+            ).start()
+        for step in range(1, count):
+            owner = lax.rem(me + count - step, count)
+            pltpu.make_async_remote_copy(
+                held.at[owner], held.at[owner], sends.at[step], recvs.at[step], {axis: owner}, MESH
+            ).wait_recv()
+        value = held[0]
+        for index in range(1, count):
+            value = value + held[index]
+        for step in range(1, count):
+            to = lax.rem(me + step, count)
+            pltpu.make_async_remote_copy(
+                held.at[me], held.at[me], sends.at[step], recvs.at[step], {axis: to}, MESH
+            ).wait_send()
+    out_ref[...] = value
+
+
+def total(value):
+    counts = [lax.axis_size(axis) for axis in AXES]
+    return pl.pallas_call(
+        total_kernel,
+        out_shape=jax.ShapeDtypeStruct(value.shape, value.dtype),
+        in_specs=[VMEM],
+        out_specs=VMEM,
+        scratch_shapes=[pltpu.VMEM((count, *value.shape), value.dtype) for count in counts]
+        + [pltpu.SemaphoreType.DMA((count,)) for count in counts] * 2,
+        compiler_params=pltpu.CompilerParams(collective_id=2, has_side_effects=True),
+    )(value)
 
 
 def shards(object_field, probe_shard, measured, positions, slot_counts):
@@ -69,12 +368,11 @@
     live = (jnp.arange(slots, dtype=jnp.int32) < slot_counts[0, 0]).astype(jnp.float32)
     live = live[:, None, None]
     anchor = jnp.zeros((), jnp.int32)
-    probes = lax.all_gather(probe_shard, "ma", axis=0, tiled=True)
+    probes, padded_object = gather(probe_shard, object_field)
     modes = probes.shape[0]
     probe_real, probe_imag = probes[None, :, 0], probes[None, :, 1]
 
-    def spectra_of(tile):
-        padded = widen(widen(tile, "gy", 2, rim), "gx", 1, rim)
+    def spectra_of(padded):
         windows = jnp.stack(
             [
                 lax.dynamic_slice(padded, (anchor, centres[s, 0], centres[s, 1]), (2, patch, patch))
@@ -117,21 +415,19 @@
             canvas = canvas + lax.dynamic_slice(
                 room[s], (anchor, rows - centres[s, 0], cols - centres[s, 1]), canvas.shape
             )
-        return lax.psum(fold(fold(canvas, "gx", 1, rim), "gy", 2, rim), "ma")
+        return settle(canvas, patch)
 
     current = object_field
-    spectra = spectra_of(current)
+    spectra = spectra_of(padded_object)
     for outer_step in range(OUTER):
         misfit = live * (mode_sum(spectra, spectra) - targets)
-        direction = -project(misfit, spectra)
+        direction, norm = project(misfit, spectra)
         moved = spectra_of(direction)
         change = 2.0 * live * mode_sum(spectra, moved)
-        sums = jnp.stack(
-            [jnp.sum(direction * direction) / lax.axis_size("ma"), jnp.sum(change * change)]
-        )
-        sums = lax.psum(sums, ("gx", "gy", "ma"))
+        curvature = jnp.zeros((8, 128), jnp.float32).at[0, 0].set(jnp.sum(change * change))
+        sums = jnp.sum(total(jnp.stack([norm, curvature])), (1, 2))
         step_size = sums[0] / (DAMPING * sums[0] + sums[1])
-        current = current + step_size * direction
+        current = current + step_size * direction[:, rim : rim + rows, rim : rim + cols]
         if outer_step + 1 < OUTER:
             spectra = spectra + step_size * moved
     return current

time: 403 us -> 236 us (0.59)
  waiting for transfers between devices: 162 us -> 0 us
  Pallas kernels: 0 us -> 143 us
  blocking collectives: 79.6 us -> 0 us
  starting transfers between devices: 39.5 us -> 0 us
  between operations: 31.9 us -> 17.5 us
  other arithmetic: 42 us -> 35.1 us
  local copies, waits for them, and re-layouts: 22.3 us -> 15.8 us
    pallas_call x0 -> x5, Pallas kernels: none -> 143 us  [the longest x2 67.3 us: settle(): pl.pallas_call(functools.partial(settle_kernel, rim), out_shape=(jax.Shap...]
    psum x2 -> x0, blocking collectives: 79.6 us -> none  [shards(): sums = lax.psum(sums, ('gx', 'gy', 'ma'))]
    psum x2 -> x0, waiting for transfers between devices: 68.5 us -> none  [project(): return lax.psum(fold(fold(canvas, 'gx', 1, rim), 'gy', 2, rim), 'ma')]
    all_gather x1 -> x0, waiting for transfers between devices: 54.5 us -> none  [shards(): probes = lax.all_gather(probe_shard, 'ma', axis=0, tiled=True)]
    ppermute x20 -> x0, starting transfers between devices: 39.4 us -> none  [the longest x10 26.1 us: shift_pair(): lax.ppermute(high_part, axis, forward)]
    ppermute x20 -> x0, waiting for transfers between devices: 37.9 us -> none  [the longest x10 30.2 us: shift_pair(): lax.ppermute(low_part, axis, backward)]
  transfers between devices with their start and end apart: 23 -> 0, of which waited for: 19 -> 0; matrix products, arithmetic and copies ran while one was open for 1% -> 0% of each run, Pallas kernels for 0% -> 0%
where the time goes in v2:
time: 236 us; the launch traced here: 235 us
  Pallas kernels  143 us (61%)
  other arithmetic  35.1 us (15%)
  matrix products  23.9 us (10%)
  between operations  17.5 us (7%)
  local copies, waits for them, and re-layouts  15.8 us (7%)
    pallas_call x2, Pallas kernels, settle(): pl.pallas_call(functools.partial(settle_kernel, rim), out_shape=(jax.Shap...  67.3 us
    pallas_call x1, Pallas kernels, gather(): pl.pallas_call(functools.partial(gather_kernel, patch // 2), out_shape=(p...  43.6 us
    pallas_call x2, Pallas kernels, total(): pl.pallas_call(total_kernel, out_shape=jax.ShapeDtypeStruct(value.shape,...  31.8 us
    dot_general x3, matrix products, spectra_of(): jnp.einsum('smcik,ckl->smil', halfway, right_two, preferred_element_type=...  16.8 us
    another operation x3, other arithmetic  11.2 us
    reduce_sum x4, other arithmetic, mode_sum(): return jnp.sum(product[..., :patch] + product[..., patch:], axis=1)  5.97 us

profile of v2, /device:TPU:0, one launch (start us, length us, event | category | flops | bytes accessed | tf_op | source)
XLA Modules:
  0.0 234.8 jit_solution(1220605279429048880)
XLA Ops:
  16.9 43.6 %shard_map.73 = (f32[8,2,256,256]{3,2,1,0:T(8,128)S(1)}, f32[2,384,512]{2,1,0:T(8,128)S(1)}) custom-call(f32[2,2,256,256]{3,2,1,0:T(8,128)S(1)} %copy-done.2, f32[2,128,256]{2,1,0:T(8,128)S(1)} %copy-done), custom_call_target="tpu_custom_call" | custom-call | tf_op jit(solution)/shard_map/pallas_call | solution.py:186
  60.5 1.7 slice_bitcast_fusion.5
  62.6 1.8 copy.24
  64.5 2.9 %copy.27 = f32[8,256,256]{1,2,0:T(8,128)} copy(f32[8,256,256]{2,1,0:T(8,128)} %get-tuple-element.58) | data formatting | bytes 4194304 | tf_op jit(solution)/shard_map/mul | solution.py:384
  67.4 4.8 %subtract_convert_fusion.2 = (bf16[2,8,1,256,256]{4,3,2,1,0:T(8,128)(2,1)}, bf16[2,8,1,256,256]{4,3,2,1,0:T(8,128)(2,1)}) fusion(f32[2,256,256]{2,1,0:T(8,128)S(1)} %get-tuple-element.70, f32[8,256,256]{2,1,0:T(8,128)} %get-tuple-element.58, f32[2,256,256]{2,1,0:T(8,128)S(1)} %get-tuple-element.69, f32[8,256,256]{2,1,0:T(8,128)S(1)} %get-tuple-element.57), kind=kLoop, calls=%fused_computation.34 | loop fusion | flops 8388608 | bytes 9437184 | tf_op jit(solution)/shard_map/convert.4
  72.1 4.9 %bitcast_multiply_fusion.4 = (f32[2,8,64,512]{3,2,1,0:T(8,128)}, f32[2,8,64,512,1]{3,2,4,1,0:T(8,128)S(1)}) fusion(bf16[2,256,512,1,1]{2,1,0,4,3:T(8,128)(2,1)} %constant.104, bf16[2,8,1,256,256]{4,3,2,1,0:T(8,128)(2,1)} %get-tuple-element.56, bf16[2,8,1,256,256]{4,3,2,1,0:T(8,128)(2,1)} %get-tuple-element.55, bf16[2,256,2,256]{3,1,2,0:T(8,128)(2,1)} %constant.101, ...), kind=kOutput, calls=%fused_computation.44 | convolution fusion | flops 1083179008 | bytes 9043972 | tf_op jit(solution)/shard_map/smcik,ckl->smil/dot_general | solution.py:389
  77.1 2.5 %fusion.24 = f32[2,64,256]{2,1,0:T(8,128)S(1)} fusion(f32[2,8,64,512]{3,2,1,0:T(8,128)} %get-tuple-element.79), kind=kLoop, calls=%fused_computation.68 | loop fusion | flops 491520 | bytes 2228224 | tf_op jit(solution)/shard_map/reduce_sum | solution.py:395
  80.6 1.7 convolution_convert_fusion.1
  83.6 2.3 convolution_bitcast_fusion.1
  86.0 1.5 add_reduce_fusion.1
  90.0 38.7 %shard_map.74 = (f32[2,384,512]{2,1,0:T(8,128)S(1)}, f32[8,128]{1,0:T(8,128)S(1)}) custom-call(f32[2,384,512]{2,1,0:T(8,128)S(1)} %add_bitcast_fusion.1.canvas_ref), custom_call_target="tpu_custom_call" | custom-call | tf_op jit(solution)/shard_map/pallas_call | solution.py:287
  129.2 3.2 %subtract_convert_fusion.1 = (bf16[2,8,1,256,256]{4,3,2,1,0:T(8,128)(2,1)}, bf16[2,8,1,256,256]{4,3,2,1,0:T(8,128)(2,1)}) fusion(f32[2,256,256]{2,1,0:T(8,128)S(1)} %get-tuple-element.68, f32[2,256,256]{2,1,0:T(8,128)S(1)} %get-tuple-element.67, f32[8,256,256]{2,1,0:T(8,128)S(1)} %copy-done.6, f32[8,256,256]{2,1,0:T(8,128)S(1)} %copy-done.4), kind=kLoop, calls=%fused_computation.30 | loop fusion | flops 8388608 | bytes 9437184 | tf_op jit(solution)/shard_map/convert.2
  132.5 6.2 %bitcast_multiply_fusion.2 = (f32[2,8,64,512]{3,2,1,0:T(8,128)}, f32[2,8,64,512,1]{3,2,4,1,0:T(8,128)}) fusion(f32[2,8,64,512,1]{3,2,4,1,0:T(8,128)} %copy-done.12, bf16[2,256,512,1,1]{2,1,0,4,3:T(8,128)(2,1)S(1)} %copy-done.16, bf16[2,8,1,256,256]{4,3,2,1,0:T(8,128)(2,1)} %get-tuple-element.54, bf16[2,8,1,256,256]{4,3,2,1,0:T(8,128)(2,1)} %get-tuple-element.53, ...), kind=kOutput, calls=%fused_computation.40 | convolution fusion | flops 1083179008 | bytes 11141124 | tf_op jit(solution)/shard_map/smcik,ckl->smil/dot_general | solution.py:389
  138.7 1.7 fusion.23
  142.3 15.8 %shard_map.75 = f32[2,8,128]{2,1,0:T(8,128)} custom-call(f32[2,8,128]{2,1,0:T(8,128)} %select_maximum_fusion.3.value_ref), custom_call_target="tpu_custom_call" | custom-call | tf_op jit(solution)/shard_map/pallas_call | solution.py:344
  161.5 3.0 %fusion.65 = (f32[2,8,64,512]{3,2,1,0:T(8,128)S(1)}, f32[2,8,64,512]{3,2,1,0:T(8,128)S(1)}) fusion(f32[2,8,64,512,1]{3,2,4,1,0:T(8,128)} %get-tuple-element.82, f32[]{:T(128)S(6)} %div.6, f32[2,8,64,512,1]{3,2,4,1,0:T(8,128)} %copy-done.12), kind=kLoop, calls=%fused_computation.126 | loop fusion | flops 1572864 | bytes 8388612 | tf_op jit(solution)/shard_map/mul | solution.py:394
  164.6 1.5 fusion.50
  166.9 2.3 convolution_bitcast_fusion
  169.3 1.5 add_reduce_fusion
  173.3 28.5 %shard_map.76 = (f32[2,384,512]{2,1,0:T(8,128)S(1)}, f32[8,128]{1,0:T(8,128)S(1)}) custom-call(f32[2,384,512]{2,1,0:T(8,128)S(1)} %add_bitcast_fusion.canvas_ref), custom_call_target="tpu_custom_call" | custom-call | tf_op jit(solution)/shard_map/pallas_call | solution.py:287
  202.3 3.2 %subtract_convert_fusion = (bf16[2,8,1,256,256]{4,3,2,1,0:T(8,128)(2,1)}, bf16[2,8,1,256,256]{4,3,2,1,0:T(8,128)(2,1)}) fusion(f32[2,256,256]{2,1,0:T(8,128)S(1)} %get-tuple-element.66, f32[2,256,256]{2,1,0:T(8,128)S(1)} %get-tuple-element.65, f32[8,256,256]{2,1,0:T(8,128)S(1)} %copy-done.7, f32[8,256,256]{2,1,0:T(8,128)S(1)} %copy-done.5), kind=kLoop, calls=%fused_computation.26 | loop fusion | flops 8388608 | bytes 9437184 | tf_op jit(solution)/shard_map/convert
  205.5 5.7 %bitcast_multiply_fusion = f32[2,8,64,512]{3,2,1,0:T(8,128)} fusion(f32[2,8,64,512]{3,2,1,0:T(8,128)} %copy-done.13, bf16[2,256,512,1,1]{2,1,0,4,3:T(8,128)(2,1)} %constant.104, bf16[2,8,1,256,256]{4,3,2,1,0:T(8,128)(2,1)} %get-tuple-element.52, bf16[2,8,1,256,256]{4,3,2,1,0:T(8,128)(2,1)} %get-tuple-element.51, bf16[2,256,2,256]{3,1,2,0:T(8,128)(2,1)} %constant.101, ...), kind=kOutput, calls=%fused_computation.37 | convolution fusion | flops 1083179008 | bytes 9043972 | tf_op jit(solution)/shard_map/smcik,ckl->smil/dot_general | solution.py:389
  211.2 1.7 fusion.21
  214.8 15.9 %shard_map.77 = f32[2,8,128]{2,1,0:T(8,128)} custom-call(f32[2,8,128]{2,1,0:T(8,128)} %select_maximum_fusion.2.value_ref), custom_call_target="tpu_custom_call" | custom-call | tf_op jit(solution)/shard_map/pallas_call | solution.py:344
  (68 shorter events, 20.4 us)
Async XLA Ops:
  14.7 1.0 copy-start
  15.6 1.2 copy-start.2
  62.2 5.2 %copy-start.3 = (f32[8,256,256]{2,1,0:T(8,128)}, f32[8,256,256]{2,1,0:T(8,128)S(1)}, u32[]{:S(2)}) copy-start(f32[8,256,256]{2,1,0:T(8,128)S(1)} %get-tuple-element.57) | copy-start | bytes 6291460
  77.0 5.2 %copy-start.12 = (f32[2,8,64,512,1]{3,2,4,1,0:T(8,128)}, f32[2,8,64,512,1]{3,2,4,1,0:T(8,128)S(1)}, u32[]{:S(2)}) copy-start(f32[2,8,64,512,1]{3,2,4,1,0:T(8,128)S(1)} %get-tuple-element.80) | copy-start | bytes 6291460
  77.1 3.5 %copy-start.14 = (bf16[512,512,1,1]{1,0,3,2:T(8,128)(2,1)S(1)}, bf16[512,512,1,1]{1,0,3,2:T(8,128)(2,1)}, u32[]{:S(2)}) copy-start(bf16[512,512,1,1]{1,0,3,2:T(8,128)(2,1)} %constant.105) | copy-start | bytes 1572868
  83.6 2.4 %copy-start.8 = (f32[8,256,256]{1,2,0:T(8,128)S(1)}, f32[8,256,256]{1,2,0:T(8,128)}, u32[]{:S(2)}) copy-start(f32[8,256,256]{1,2,0:T(8,128)} %copy.24) | copy-start | bytes 6291460
  83.6 2.4 %copy-start.10 = (f32[8,256,256]{1,2,0:T(8,128)S(1)}, f32[8,256,256]{1,2,0:T(8,128)}, u32[]{:S(2)}) copy-start(f32[8,256,256]{1,2,0:T(8,128)} %copy.27) | copy-start | bytes 6291460
  90.0 39.2 %copy-start.4 = (f32[8,256,256]{2,1,0:T(8,128)S(1)}, f32[8,256,256]{2,1,0:T(8,128)}, u32[]{:S(2)}) copy-start(f32[8,256,256]{2,1,0:T(8,128)} %copy-done.3) | copy-start | bytes 6291460
  90.0 39.2 %copy-start.6 = (f32[8,256,256]{2,1,0:T(8,128)S(1)}, f32[8,256,256]{2,1,0:T(8,128)}, u32[]{:S(2)}) copy-start(f32[8,256,256]{2,1,0:T(8,128)} %get-tuple-element.58) | copy-start | bytes 6291460
  129.2 3.3 %copy-start.16 = (bf16[2,256,512,1,1]{2,1,0,4,3:T(8,128)(2,1)S(1)}, bf16[2,256,512,1,1]{2,1,0,4,3:T(8,128)(2,1)}, u32[]{:S(2)}) copy-start(bf16[2,256,512,1,1]{2,1,0,4,3:T(8,128)(2,1)} %constant.104) | copy-start | bytes 1572868
  164.4 2.5 %copy-start.13 = (f32[2,8,64,512]{3,2,1,0:T(8,128)}, f32[2,8,64,512]{3,2,1,0:T(8,128)S(1)}, u32[]{:S(2)}) copy-start(f32[2,8,64,512]{3,2,1,0:T(8,128)S(1)} %get-tuple-element.46) | copy-start | bytes 6291460
  164.4 1.7 copy-start.15
  166.9 2.4 %copy-start.9 = (f32[8,256,256]{1,2,0:T(8,128)S(1)}, f32[8,256,256]{1,2,0:T(8,128)}, u32[]{:S(2)}) copy-start(f32[8,256,256]{1,2,0:T(8,128)} %copy.24) | copy-start | bytes 6291460
  166.9 2.4 %copy-start.11 = (f32[8,256,256]{1,2,0:T(8,128)S(1)}, f32[8,256,256]{1,2,0:T(8,128)}, u32[]{:S(2)}) copy-start(f32[8,256,256]{1,2,0:T(8,128)} %copy.27) | copy-start | bytes 6291460
  173.3 29.0 %copy-start.5 = (f32[8,256,256]{2,1,0:T(8,128)S(1)}, f32[8,256,256]{2,1,0:T(8,128)}, u32[]{:S(2)}) copy-start(f32[8,256,256]{2,1,0:T(8,128)} %copy-done.3) | copy-start | bytes 6291460
  173.3 29.0 %copy-start.7 = (f32[8,256,256]{2,1,0:T(8,128)S(1)}, f32[8,256,256]{2,1,0:T(8,128)}, u32[]{:S(2)}) copy-start(f32[8,256,256]{2,1,0:T(8,128)} %get-tuple-element.58) | copy-start | bytes 6291460
  205.5 28.5 %copy-start.1 = (f32[2,128,256]{2,1,0:T(8,128)S(1)}, f32[2,128,256]{2,1,0:T(8,128)}, u32[]{:S(2)}) copy-start(f32[2,128,256]{2,1,0:T(8,128)} %tile_ref.1) | copy-start | bytes 786436

commit v3 on v2

--- a/solution.py
+++ b/solution.py
@@ -13,15 +13,24 @@
 DAMPING = 1.0
 
 
-def dft_tables(patch_width):
-    ladder = np.arange(patch_width)
-    angles = (ladder[:, None] * ladder[None, :] % patch_width) * (2.0 * math.pi / patch_width)
-    factor = 1.0 / math.sqrt(patch_width)
+def dft_tables(patch, groups):
+    ladder = np.arange(patch)
+    angles = (ladder[:, None] * ladder[None, :] % patch) * (2.0 * math.pi / patch)
+    factor = 1.0 / math.sqrt(patch)
     real_part = np.cos(angles) * factor
     imag_part = -np.sin(angles) * factor
-    table_one = np.block([[real_part, -imag_part], [imag_part, real_part]])
-    table_two = np.block([[real_part, imag_part], [-imag_part, real_part]])
-    return jnp.asarray(table_one, jnp.bfloat16), jnp.asarray(table_two, jnp.bfloat16)
+    one = np.block([[real_part, -imag_part], [imag_part, real_part]])
+    two = np.block([[real_part, imag_part], [-imag_part, real_part]])
+    share = patch // groups
+    left_one = one.reshape(2, groups, share, 2 * patch).transpose(1, 0, 2, 3)
+    left_two = two.reshape(2 * patch, 2, groups, share).transpose(2, 0, 1, 3)
+    parts = (
+        left_one.reshape(groups, 2 * share, 2 * patch),
+        two,
+        one,
+        left_two.reshape(groups, 2 * patch, 2 * share),
+    )
+    return tuple(jnp.asarray(part, jnp.bfloat16) for part in parts)
 
 
 MESH = pl.DeviceIdType.MESH
@@ -352,84 +361,203 @@
     )(value)
 
 
+SMEM = pl.BlockSpec(memory_space=pltpu.SMEM)
+
+
+def aligned_rows(row, patch):
+    base = row // 8
+    return pl.ds(pl.multiple_of(base * 8, 8), patch + 8), row - base * 8
+
+
+def transform_slot(slot, centres, padded_ref, probes_ref, left, right, spectra_ref, window, stack):
+    modes, _, patch, _ = probes_ref.shape
+    share = left.shape[0] // 2
+    width = padded_ref.shape[2]
+    shift = lax.rem(width - centres[slot, 1], width)
+    rows, offset = aligned_rows(centres[slot, 0], patch)
+    tall = patch + 8
+    for part in range(2):
+        band = pltpu.roll(padded_ref[part, rows, :], shift, 1)[:, :patch]
+        window[part] = pltpu.roll(band, lax.rem(tall - offset, tall), 0)[:patch]
+
+    def one_mode(mode, carry):
+        probe_real, probe_imag = probes_ref[mode, 0], probes_ref[mode, 1]
+        real = (probe_real * window[0] - probe_imag * window[1]).astype(jnp.bfloat16)
+        imag = (probe_real * window[1] + probe_imag * window[0]).astype(jnp.bfloat16)
+        half = jnp.dot(
+            left, jnp.concatenate([real, imag], 0), preferred_element_type=jnp.float32
+        ).astype(jnp.bfloat16)
+        rows = pl.ds(pl.multiple_of(mode * share, share), share)
+        stack[rows, :] = jnp.concatenate([half[:share], half[share:]], 1)
+        return carry
+
+    lax.fori_loop(0, modes, one_mode, 0, unroll=2)
+    result = jnp.dot(stack[...], right, preferred_element_type=jnp.float32)
+    for mode in range(modes):
+        spectra_ref[slot, mode] = result[mode * share : (mode + 1) * share]
+
+
+def project_slot(slot, centres, weights, spectra_ref, probes_ref, table, left, canvas, piece, stack):
+    modes, _, patch, _ = probes_ref.shape
+    share = weights.shape[0]
+    width = canvas.shape[2]
+    doubled = jnp.concatenate([weights, weights], 1)
+    for mode in range(modes):
+        stack[mode * share : (mode + 1) * share] = (
+            2.0 * spectra_ref[slot, mode] * doubled
+        ).astype(jnp.bfloat16)
+    turned = jnp.dot(stack[...], table, preferred_element_type=jnp.float32)
+    stack[...] = turned.astype(jnp.bfloat16)
+    piece[...] = jnp.zeros(piece.shape, jnp.float32)
+
+    def one_mode(mode, carry):
+        rows = stack[pl.ds(pl.multiple_of(mode * share, share), share), :]
+        back = jnp.dot(
+            left,
+            jnp.concatenate([rows[:, :patch], rows[:, patch:]], 0),
+            preferred_element_type=jnp.float32,
+        )
+        real, imag = back[:patch], back[patch:]
+        probe_real, probe_imag = probes_ref[mode, 0], probes_ref[mode, 1]
+        piece[0] += probe_real * real + probe_imag * imag
+        piece[1] += probe_real * imag - probe_imag * real
+        return carry
+
+    lax.fori_loop(0, modes, one_mode, 0, unroll=2)
+    rows, offset = aligned_rows(centres[slot, 0], patch)
+    low = jnp.zeros((8, patch), jnp.float32)
+    blank = jnp.zeros((patch + 8, width - patch), jnp.float32)
+    for part in range(2):
+        moved = pltpu.roll(jnp.concatenate([piece[part], low], 0), offset, 0)
+        moved = pltpu.roll(jnp.concatenate([moved, blank], 1), centres[slot, 1], 1)
+        canvas[part, rows, :] += moved
+
+
+def misfit_of(slot, counts, measured_ref, spectra_ref):
+    modes, share, double = spectra_ref.shape[1:]
+    patch = double // 2
+    intensity = jnp.zeros((share, patch), jnp.float32)
+    for mode in range(modes):
+        spectrum = spectra_ref[slot, mode]
+        square = spectrum * spectrum
+        intensity = intensity + (square[:, :patch] + square[:, patch:])
+    first = pl.multiple_of(lax.axis_index("ma") * share, share)
+    live = jnp.where(slot < counts[0, 0], 1.0, 0.0)
+    return live * (intensity - measured_ref[slot, pl.ds(first, share), :])
+
+
+def first_kernel(
+    centres, counts, padded_ref, probes_ref, measured_ref, left_one, right, table, left_two,
+    spectra_ref, canvas, window, stack,
+):
+    group = lax.axis_index("ma")
+    canvas[...] = jnp.zeros(canvas.shape, jnp.float32)
+    for slot in range(measured_ref.shape[0]):
+        transform_slot(
+            slot, centres, padded_ref, probes_ref, left_one[group], right[...],
+            spectra_ref, window, stack,
+        )
+        weights = misfit_of(slot, counts, measured_ref, spectra_ref)
+        project_slot(
+            slot, centres, weights, spectra_ref, probes_ref, table[...], left_two[group],
+            canvas, window, stack,
+        )
+
+
+def later_kernel(
+    centres, counts, sums_ref, old_ref, moved_ref, probes_ref, measured_ref, table, left_two,
+    spectra_ref, canvas, window, stack,
+):
+    group = lax.axis_index("ma")
+    norm = jnp.sum(sums_ref[0], keepdims=True)
+    step_size = norm / (DAMPING * norm + jnp.sum(sums_ref[1], keepdims=True))
+    canvas[...] = jnp.zeros(canvas.shape, jnp.float32)
+    for slot in range(measured_ref.shape[0]):
+        for mode in range(probes_ref.shape[0]):
+            spectra_ref[slot, mode] = old_ref[slot, mode] + step_size * moved_ref[slot, mode]
+        weights = misfit_of(slot, counts, measured_ref, spectra_ref)
+        project_slot(
+            slot, centres, weights, spectra_ref, probes_ref, table[...], left_two[group],
+            canvas, window, stack,
+        )
+
+
+def change_kernel(
+    centres, counts, padded_ref, probes_ref, spectra_ref, norm_ref, left_one, right,
+    moved_ref, sums_ref, window, stack,
+):
+    group = lax.axis_index("ma")
+    slots, modes, share, double = spectra_ref.shape
+    patch = double // 2
+    curvature = jnp.zeros((8, 128), jnp.float32)
+    for slot in range(slots):
+        transform_slot(
+            slot, centres, padded_ref, probes_ref, left_one[group], right[...],
+            moved_ref, window, stack,
+        )
+        change = jnp.zeros((share, patch), jnp.float32)
+        for mode in range(modes):
+            product = spectra_ref[slot, mode] * moved_ref[slot, mode]
+            change = change + (product[:, :patch] + product[:, patch:])
+        live = jnp.where(slot < counts[0, 0], 2.0, 0.0)
+        change = live * change
+        curvature = curvature + fold_rows(change * change)
+    sums_ref[0] = norm_ref[...]
+    sums_ref[1] = curvature
+
+
+def local_call(kernel, operands, shapes, patch, share, modes):
+    f32 = jnp.float32
+    return pl.pallas_call(
+        kernel,
+        out_shape=tuple(jax.ShapeDtypeStruct(shape, f32) for shape in shapes),
+        in_specs=[SMEM, SMEM] + [VMEM] * (len(operands) - 2),
+        out_specs=(VMEM,) * len(shapes),
+        scratch_shapes=[
+            pltpu.VMEM((2, patch, patch), f32),
+            pltpu.VMEM((modes * share, 2 * patch), jnp.bfloat16),
+        ],
+        compiler_params=pltpu.CompilerParams(vmem_limit_bytes=48 << 20),
+    )(*operands)
+
+
 def shards(object_field, probe_shard, measured, positions, slot_counts):
     patch = probe_shard.shape[-1]
     rim = patch // 2
     rows, cols = object_field.shape[1:]
     slots = measured.shape[2]
-    share = patch // lax.axis_size("ma")
-    first = lax.axis_index("ma") * share
-    table_one, table_two = dft_tables(patch)
-    left_one = lax.dynamic_slice_in_dim(table_one.reshape(2, patch, 2, patch), first, share, 1)
-    right_two = table_two.reshape(2, patch, 2 * patch)
-    left_two = lax.dynamic_slice_in_dim(table_two.reshape(2, patch, 2, patch), first, share, 3)
-    targets = lax.dynamic_slice_in_dim(measured[0, 0], first, share, 1)
-    centres = positions[0, 0]
-    live = (jnp.arange(slots, dtype=jnp.int32) < slot_counts[0, 0]).astype(jnp.float32)
-    live = live[:, None, None]
-    anchor = jnp.zeros((), jnp.int32)
+    groups = lax.axis_size("ma")
+    share = patch // groups
+    modes = probe_shard.shape[0] * groups
+    left_one, right, table, left_two = dft_tables(patch, groups)
+    targets, centres = measured[0, 0], positions[0, 0]
     probes, padded_object = gather(probe_shard, object_field)
-    modes = probes.shape[0]
-    probe_real, probe_imag = probes[None, :, 0], probes[None, :, 1]
-
-    def spectra_of(padded):
-        windows = jnp.stack(
-            [
-                lax.dynamic_slice(padded, (anchor, centres[s, 0], centres[s, 1]), (2, patch, patch))
-                for s in range(slots)
-            ]
-        )
-        real, imag = windows[:, None, 0], windows[:, None, 1]
-        waves = jnp.stack(
-            [probe_real * real - probe_imag * imag, probe_real * imag + probe_imag * real], 2
-        ).astype(jnp.bfloat16)
-        halfway = jnp.einsum(
-            "pqci,smcik->smpqk", left_one, waves, preferred_element_type=jnp.float32
-        ).astype(jnp.bfloat16)
-        return jnp.einsum(
-            "smcik,ckl->smil", halfway, right_two, preferred_element_type=jnp.float32
-        )
-
-    def mode_sum(first_spectra, second_spectra):
-        product = first_spectra * second_spectra
-        return jnp.sum(product[..., :patch] + product[..., patch:], axis=1)
-
-    def project(weights, spectra):
-        doubled = jnp.concatenate([weights, weights], -1)[:, None]
-        scaled = (2.0 * spectra * doubled).astype(jnp.bfloat16)
-        turned = jnp.einsum(
-            "smik,kl->smil", scaled, table_one, preferred_element_type=jnp.float32
-        ).astype(jnp.bfloat16)
-        back = jnp.einsum(
-            "pqci,smicl->smpql",
-            left_two,
-            turned.reshape(slots, modes, share, 2, patch),
-            preferred_element_type=jnp.float32,
-        )
-        real = jnp.sum(probe_real * back[:, :, 0] + probe_imag * back[:, :, 1], axis=1)
-        imag = jnp.sum(probe_real * back[:, :, 1] - probe_imag * back[:, :, 0], axis=1)
-        pieces = jnp.stack([real, imag], 1)
-        canvas = jnp.zeros((2, rows + patch, cols + patch), jnp.float32)
-        room = jnp.pad(pieces, ((0, 0), (0, 0), (rows, rows), (cols, cols)))
-        for s in range(slots):
-            canvas = canvas + lax.dynamic_slice(
-                room[s], (anchor, rows - centres[s, 0], cols - centres[s, 1]), canvas.shape
+    spectra_shape = (slots, modes, share, 2 * patch)
+    run = functools.partial(local_call, patch=patch, share=share, modes=modes)
+    current = object_field
+    for outer_step in range(OUTER):
+        if outer_step == 0:
+            spectra, canvas = run(
+                first_kernel,
+                (centres, slot_counts, padded_object, probes, targets, left_one, right, table, left_two),
+                (spectra_shape, padded_object.shape),
             )
-        return settle(canvas, patch)
-
-    current = object_field
-    spectra = spectra_of(padded_object)
-    for outer_step in range(OUTER):
-        misfit = live * (mode_sum(spectra, spectra) - targets)
-        direction, norm = project(misfit, spectra)
-        moved = spectra_of(direction)
-        change = 2.0 * live * mode_sum(spectra, moved)
-        curvature = jnp.zeros((8, 128), jnp.float32).at[0, 0].set(jnp.sum(change * change))
-        sums = jnp.sum(total(jnp.stack([norm, curvature])), (1, 2))
-        step_size = sums[0] / (DAMPING * sums[0] + sums[1])
+        else:
+            spectra, canvas = run(
+                later_kernel,
+                (centres, slot_counts, sums, spectra, moved, probes, targets, table, left_two),
+                (spectra_shape, padded_object.shape),
+            )
+        direction, norm = settle(canvas, patch)
+        moved, sums = run(
+            change_kernel,
+            (centres, slot_counts, direction, probes, spectra, norm, left_one, right),
+            (spectra_shape, (2, 8, 128)),
+        )
+        sums = total(sums)
+        norms = jnp.sum(sums, (1, 2))
+        step_size = norms[0] / (DAMPING * norms[0] + norms[1])
         current = current + step_size * direction[:, rim : rim + rows, rim : rim + cols]
-        if outer_step + 1 < OUTER:
-            spectra = spectra + step_size * moved
     return current
 
 

time: 236 us -> 206 us (0.87)
  Pallas kernels: 143 us -> 179 us
  other arithmetic: 35.1 us -> 2.61 us
  matrix products: 23.9 us -> 0 us
  between operations: 17.5 us -> 4.64 us
  local copies, waits for them, and re-layouts: 15.8 us -> 18.4 us
    pallas_call x0 -> x4, Pallas kernels: none -> 36.9 us  [local_call(): pl.pallas_call(kernel, out_shape=tuple((jax.ShapeDtypeStruct(shape, f32)...]
    dot_general x7 -> x0, matrix products: 23.9 us -> none  [the longest x3 16.8 us: spectra_of(): jnp.einsum('smcik,ckl->smil', halfway, right_two, preferred_element_type=...]
    unnamed x34 -> x46, local copies, waits for them, and re-layouts: 2.24 us -> 17.2 us
    another operation x7 -> x0, other arithmetic: 14.6 us -> none
    reduce_sum x10 -> x2, other arithmetic: 12.1 us -> 0.89 us  [shards(): norms = jnp.sum(sums, (1, 2))]
    mul x3 -> x0, local copies, waits for them, and re-layouts: 6.47 us -> none  [the longest x2 3.55 us: project(): probe_real * back[:, :, 0] + probe_imag * back[:, :, 1]]
    mul x9 -> x0, other arithmetic: 5.76 us -> none  [the longest x1 2.96 us: mode_sum(): product = first_spectra * second_spectra]
    slice x5 -> x2, local copies, waits for them, and re-layouts: 3.89 us -> 1.17 us  [shards(): step_size = norms[0] / (DAMPING * norms[0] + norms[1])]
where the time goes in v3:
time: 206 us; the launch traced here: 205 us
  Pallas kernels  179 us (87%)
  local copies, waits for them, and re-layouts  18.4 us (9%)
  between operations  4.64 us (2%)
  other arithmetic  2.61 us (1%)
    pallas_call x2, Pallas kernels, settle(): pl.pallas_call(functools.partial(settle_kernel, rim), out_shape=(jax.Shap...  67.2 us
    pallas_call x1, Pallas kernels, gather(): pl.pallas_call(functools.partial(gather_kernel, patch // 2), out_shape=(p...  43.6 us
    pallas_call x4, Pallas kernels, local_call(): pl.pallas_call(kernel, out_shape=tuple((jax.ShapeDtypeStruct(shape, f32)...  36.9 us
    pallas_call x2, Pallas kernels, total(): pl.pallas_call(total_kernel, out_shape=jax.ShapeDtypeStruct(value.shape,...  31.6 us
    unnamed x46, local copies, waits for them, and re-layouts  17.2 us

profile of v3, /device:TPU:0, one launch (start us, length us, event | category | flops | bytes accessed | tf_op | source)
XLA Modules:
  0.0 204.9 jit_solution(1370150585391530289)
XLA Ops:
  0.8 0.9 copy-done.14
  1.7 1.2 copy-done.16
  2.9 43.6 %shard_map.91 = (f32[8,2,256,256]{3,2,1,0:T(8,128)S(1)}, f32[2,384,512]{2,1,0:T(8,128)S(1)}) custom-call(f32[2,2,256,256]{3,2,1,0:T(8,128)S(1)} %copy-done.16, f32[2,128,256]{2,1,0:T(8,128)S(1)} %copy-done.14), custom_call_target="tpu_custom_call" | custom-call | tf_op jit(solution)/shard_map/pallas_call | solution.py:195
  46.5 1.9 copy-done
  48.5 1.0 copy-done.5
  49.5 1.0 copy-done.7
  50.6 1.0 copy-done.9
  52.3 12.3 %shard_map.92 = (f32[2,8,64,512]{3,2,1,0:T(8,128)}, f32[2,384,512]{2,1,0:T(8,128)S(1)}) custom-call(s32[2,2]{1,0:T(2,128)S(1)} %bitcast.8, s32[1,1]{1,0:T(1,128)S(6)} %copy.10.counts, f32[2,384,512]{2,1,0:T(8,128)S(1)} %get-tuple-element.18.padded_ref, f32[8,2,256,256]{3,2,1,0:T(8,128)} %copy-done, f32[2,256,256]{2,1,0:T(8,128)S(1)} %bitcast.6, ...), custom_call_target="tpu_custom_call" | custom-call | tf_op jit(solution)/shard_map/pallas_call | solution.py:511
  64.6 38.7 %shard_map.93 = (f32[2,384,512]{2,1,0:T(8,128)S(1)}, f32[8,128]{1,0:T(8,128)S(1)}) custom-call(f32[2,384,512]{2,1,0:T(8,128)S(1)} %get-tuple-element.20.canvas_ref), custom_call_target="tpu_custom_call" | custom-call | tf_op jit(solution)/shard_map/pallas_call | solution.py:296
  103.3 7.1 %shard_map.94 = (f32[2,8,64,512]{3,2,1,0:T(8,128)S(1)}, f32[2,8,128]{2,1,0:T(8,128)S(1)}) custom-call(s32[2,2]{1,0:T(2,128)S(1)} %bitcast.9, s32[1,1]{1,0:T(1,128)S(6)} %copy.10.counts, f32[2,384,512]{2,1,0:T(8,128)S(1)} %get-tuple-element.21.padded_ref, f32[8,2,256,256]{3,2,1,0:T(8,128)} %copy-done, ...), custom_call_target="tpu_custom_call" | custom-call | tf_op jit(solution)/shard_map/pallas_call | solution.py:511
  110.4 1.4 copy-done.11
  112.4 15.8 %shard_map.95.sums_ref = f32[2,8,128]{2,1,0:T(8,128)} custom-call(f32[2,8,128]{2,1,0:T(8,128)} %copy-done.22), custom_call_target="tpu_custom_call" | custom-call | tf_op jit(solution)/shard_map/pallas_call | solution.py:353
  128.2 1.0 copy-done.8
  129.2 1.0 copy-done.10
  130.3 0.7 copy-done.17
  131.0 8.5 %shard_map.96 = (f32[2,8,64,512]{3,2,1,0:T(8,128)S(1)}, f32[2,384,512]{2,1,0:T(8,128)S(1)}) custom-call(s32[2,2]{1,0:T(2,128)S(1)} %bitcast.10, s32[1,1]{1,0:T(1,128)S(6)} %copy.10.counts, f32[2,8,128]{2,1,0:T(8,128)S(1)} %copy-done.17, f32[2,8,64,512]{3,2,1,0:T(8,128)} %get-tuple-element.22.spectra_ref.old_ref, f32[2,8,64,512]{3,2,1,0:T(8,128)} %copy-done.11, ...), custom_call_target="tpu_custom_call" | custom-call | tf_op jit(solution)/shard_map/pallas_call | solution.py:511
  139.5 1.4 copy-done.4
  140.8 1.1 copy-done.12
  144.6 1.4 copy-done.13
  146.0 28.5 %shard_map.97 = (f32[2,384,512]{2,1,0:T(8,128)S(1)}, f32[8,128]{1,0:T(8,128)S(1)}) custom-call(f32[2,384,512]{2,1,0:T(8,128)S(1)} %copy-done.13), custom_call_target="tpu_custom_call" | custom-call | tf_op jit(solution)/shard_map/pallas_call | solution.py:296
  174.5 9.0 %shard_map.98 = (f32[2,8,64,512]{3,2,1,0:T(8,128)}, f32[2,8,128]{2,1,0:T(8,128)S(1)}) custom-call(s32[2,2]{1,0:T(2,128)S(1)} %bitcast.11, s32[1,1]{1,0:T(1,128)S(6)} %copy.10.counts, f32[2,384,512]{2,1,0:T(8,128)S(1)} %get-tuple-element.27.padded_ref, f32[8,2,256,256]{3,2,1,0:T(8,128)} %copy-done, f32[2,8,64,512]{3,2,1,0:T(8,128)} %copy-done.4, ...), custom_call_target="tpu_custom_call" | custom-call | tf_op jit(solution)/shard_map/pallas_call | solution.py:511
  184.1 15.9 %shard_map.99 = f32[2,8,128]{2,1,0:T(8,128)} custom-call(f32[2,8,128]{2,1,0:T(8,128)} %copy-done.21), custom_call_target="tpu_custom_call" | custom-call | tf_op jit(solution)/shard_map/pallas_call | solution.py:353
  200.0 0.8 reduce_sum.19
  203.2 1.7 multiply_add_fusion
  (36 shorter events, 3.2 us)
Async XLA Ops:
  0.0 48.5 %copy-start.1 = (bf16[512,512]{1,0:T(8,128)(2,1)S(1)}, bf16[512,512]{1,0:T(8,128)(2,1)}, u32[]{:S(2)}) copy-start(bf16[512,512]{1,0:T(8,128)(2,1)} %constant.11.clone.right) | copy-start | bytes 1572868
  0.0 48.5 %copy-start.2 = (bf16[4,128,512]{2,1,0:T(8,128)(2,1)S(1)}, bf16[4,128,512]{2,1,0:T(8,128)(2,1)}, u32[]{:S(2)}) copy-start(bf16[4,128,512]{2,1,0:T(8,128)(2,1)} %constant.10.clone.left_one) | copy-start | bytes 1572868
  0.7 1.0 copy-start.14
  1.7 1.2 copy-start.16
  46.5 1.9 copy-start
  48.5 1.0 copy-start.5
  49.5 1.0 copy-start.7
  50.6 1.0 copy-start.9
  51.6 0.7 copy-start.19
  103.3 24.9 %copy-start.6 = (f32[1,1,2,256,256]{4,3,2,1,0:T(8,128)S(1)}, f32[1,1,2,256,256]{4,3,2,1,0:T(8,128)}, u32[]{:S(2)}) copy-start(f32[1,1,2,256,256]{4,3,2,1,0:T(8,128)} %param.11) | copy-start | bytes 1572868
  103.3 24.9 %copy-start.20 = (s32[1,1,2,2]{3,2,1,0:T(2,128)S(1)}, s32[1,1,2,2]{3,2,1,0:T(2,128)}, u32[]{:S(2)}) copy-start(s32[1,1,2,2]{3,2,1,0:T(2,128)} %param.12) | copy-start | bytes 52
  110.4 1.4 copy-start.11
  111.8 0.6 copy-start.22
  128.2 1.0 copy-start.8
  129.2 1.0 copy-start.10
  130.3 0.7 copy-start.17
  131.0 11.0 %copy-start.18 = (f32[2,8,128]{2,1,0:T(8,128)S(1)}, f32[2,8,128]{2,1,0:T(8,128)}, u32[]{:S(2)}) copy-start(f32[2,8,128]{2,1,0:T(8,128)} %shard_map.95.sums_ref) | copy-start | bytes 24580
  139.4 1.4 copy-start.4
  140.8 1.1 copy-start.12
  144.6 1.4 copy-start.13
  174.5 9.0 %copy-start.3 = (f32[2,384,512]{2,1,0:T(8,128)}, f32[2,384,512]{2,1,0:T(8,128)S(1)}, u32[]{:S(2)}) copy-start(f32[2,384,512]{2,1,0:T(8,128)S(1)} %get-tuple-element.27.padded_ref) | copy-start | bytes 4718596
  174.5 28.7 %copy-start.15 = (f32[2,128,256]{2,1,0:T(8,128)S(1)}, f32[2,128,256]{2,1,0:T(8,128)}, u32[]{:S(2)}) copy-start(f32[2,128,256]{2,1,0:T(8,128)} %tile_ref.1) | copy-start | bytes 786436
  183.5 0.6 copy-start.21
